TPU v7x, 32 devices: a whole 2x2x4 slice. The times are simulated.
32 devices in a mesh: silo: 4 (over z), row: 8 (over y, x, core).
Axes of the slice: x: 2, y: 2, z: 4, core: 2. Of those that a mesh axis runs over, the one named last changes fastest.
Arguments:
- silo_grams: float32 [8, 4096, 4096], P('silo', 'row'), may hold values from -9 to 81, as said below
- silo_weights: bfloat16 [8, 4096, 640], P('silo', 'row'), may hold values from -6 to 6
Outputs:
- merged_rows: float32 [640, 4096], P(('silo', 'row'))
Inputs may be any that keep to these rules, and one draw needn't show every extreme that they name: `silo_grams`: each silo's Gram is symmetric up to float32 rounding and positive definite.
All inputs are finite; a program needn't handle non-finite values.
Results may differ from a plain program's by a relative error of at most 0.0003.
Values may be sent and summed in bfloat16 or wider, within the bound.
No kernel may reach another device: no remote copies, remote signals or barrier semaphores. Data moves between devices by JAX's collectives and lax.ppermute only.
A program may use at most 128 MiB of HBM per device.

v0:
```python
import jax
import jax.numpy as jnp
from jax import lax
from jax.sharding import PartitionSpec as P

ITERS = 2


full_precision = lax.Precision.HIGHEST


def conj_grad(right_side, apply_op, sum_squares, sum_curv):
    solution = jnp.zeros_like(right_side)
    residual = right_side
    direction = right_side
    res_norm = sum_squares(jnp.sum(residual * residual, axis=0))
    for iteration in range(ITERS):
        mapped = apply_op(direction)
        step_size = res_norm / sum_curv(jnp.sum(direction * mapped, axis=0))
        solution = solution + step_size * direction
        residual = residual - step_size * mapped
        if iteration + 1 < ITERS:
            next_norm = sum_squares(jnp.sum(residual * residual, axis=0))
            direction = residual + next_norm / res_norm * direction
            res_norm = next_norm
    return solution


def local(silo_grams, silo_weights):
    partial_op = jnp.sum(silo_grams, axis=0)
    partial_rhs = jnp.einsum(
        "srk,skc->rc",
        silo_grams,
        lax.all_gather(silo_weights, "row", axis=1, tiled=True).astype(jnp.float32),
        precision=full_precision,
    )
    operator = lax.psum(partial_op, "silo")
    right_side = lax.psum_scatter(partial_rhs, "silo", scatter_dimension=1, tiled=True)

    def apply_cols(direction):
        return jnp.dot(
            operator, lax.all_gather(direction, "row", axis=0, tiled=True), precision=full_precision
        )

    def squares_cols(values):
        return lax.psum(values, "row")

    def curv_values(values):
        return lax.psum(values, "row")

    solution = conj_grad(right_side, apply_cols, squares_cols, curv_values)
    transposed = solution.T
    return lax.all_to_all(transposed, "row", split_axis=0, concat_axis=1, tiled=True)


def solution(mesh):
    placed = (P("silo", "row", None), P("silo", "row", None))
    return jax.shard_map(
        local, mesh=mesh, in_specs=placed, out_specs=P(("silo", "row"), None), check_vma=False
    )
```

profile of v0, /device:TPU:0, one launch (start us, length us, event | category | flops | bytes accessed | tf_op | source)
XLA Modules:
  0.0 567.5 jit_solution(10931932025676428913)
XLA Ops:
  6.5 0.0 all-gather.4.cloned.1.call-start
  6.5 2.4 copy.6
  9.0 0.0 all-gather.4.cloned.1.call-update
  9.0 0.0 reduce-scatter.2.cloned.1.call-start
  9.0 68.1 %all-gather.4.cloned.1.call-done = bf16[2,4096,640]{1,2,0:T(8,128)(2,1)} async-done(((bf16[2,512,640]{1,2,0:T(8,128)(2,1)}), bf16[2,4096,640]{1,2,0:T(8,128)(2,1)}) %all-gather.4.cloned.1.call-update) | async-done | bytes 10485776 | tf_op jit(solution)/shard_map/all_gather | solution.py:34
  77.1 21.3 %convolution_bitcast_fusion = f32[512,640]{0,1:T(8,128)} fusion(f32[2,512,4096]{2,1,0:T(8,128)} %param.2, bf16[2,4096,640]{1,2,0:T(8,128)(2,1)} %all-gather.4.cloned.1.call-done), kind=kOutput, calls=%fused_computation | convolution fusion | flops 32212254720 | bytes 28573696 | tf_op jit(solution)/shard_map/srk,skc->rc/dot_general | solution.py:31
  98.4 0.0 reduce-scatter.2.cloned.1.call-update
  98.5 0.0 all-reduce.3.cloned.1.call-start
  98.5 11.6 %reduce_sum.46 = f32[512,4096]{1,0:T(8,128)} reduce(f32[2,512,4096]{2,1,0:T(8,128)} %param.2, f32[]{:T(128)} %constant.0.clone.1), dimensions={0}, to_apply=%region_3.0 | reduce | flops 2097152 | bytes 25165828 | tf_op jit(solution)/shard_map/reduce_sum | solution.py:30
  110.1 0.0 all-reduce.3.cloned.1.call-update
  110.1 0.0 all-gather.6.cloned.1.call-start
  110.2 19.8 %reduce-scatter.2.cloned.1.call-done = f32[512,160]{0,1:T(8,128)} async-done(((f32[512,640]{0,1:T(8,128)}), f32[512,160]{0,1:T(8,128)}) %reduce-scatter.2.cloned.1.call-update) | async-done | bytes 327696 | tf_op jit(solution)/shard_map/reduce_scatter | solution.py:38
  130.0 0.0 copy-start
  130.0 0.0 all-gather.6.cloned.1.call-update
  130.0 0.2 all-gather.8.cloned.1.call-start
  130.2 291.8 %all-reduce.3.cloned.1.call-done = f32[512,4096]{1,0:T(8,128)} async-done(((f32[512,4096]{1,0:T(8,128)}), f32[512,4096]{1,0:T(8,128)}) %all-reduce.3.cloned.1.call-update) | async-done | bytes 8388624 | tf_op jit(solution)/shard_map/psum | solution.py:37
  422.0 30.8 %all-gather.6.cloned.1.call-done = f32[4096,160]{0,1:T(8,128)} async-done(((f32[512,160]{0,1:T(8,128)}), f32[4096,160]{0,1:T(8,128)}) %all-gather.6.cloned.1.call-update) | async-done | bytes 2621456 | tf_op jit(solution)/shard_map/all_gather | solution.py:42
  452.8 13.3 %multiply_reduce_fusion.1 = (f32[160]{0:T(256)S(1)}, f32[160]{0:T(256)S(1)}, f32[512,160]{0,1:T(8,128)S(1)}) fusion(f32[512,160]{0,1:T(8,128)} %reduce-scatter.2.cloned.1.call-done, f32[512,4096]{1,0:T(8,128)} %all-reduce.3.cloned.1.call-done, f32[4096,160]{0,1:T(8,128)} %all-gather.6.cloned.1.call-done), kind=kOutput, calls=%fused_computation.7 | convolution fusion | flops 4026859264 | bytes 11666688 | tf_op jit(solution)/shard_map/dot_general | solution.py:41
  466.0 13.1 %all-reduce = (f32[160]{0:T(256)S(1)}, f32[160]{0:T(256)S(1)}) all-reduce(f32[160]{0:T(256)S(1)} %get-tuple-element.6, f32[160]{0:T(256)S(1)} %get-tuple-element.5), channel_id=1, replica_groups=mesh['silo'=4,'row'=8] {'row'}, use_global_device_ids=true, to_apply=%region_2.0 | all-reduce | flops 320 | bytes 2560 | tf_op jit(solution)/shard_map/psum | solution.py:46
  479.1 0.0 copy-done
  479.1 0.2 multiply_reduce_fusion
  479.3 12.0 %psum.38 = f32[160]{0:T(256)S(1)} all-reduce(f32[160]{0:T(256)S(1)} %multiply_reduce_fusion), channel_id=1, replica_groups=mesh['silo'=4,'row'=8] {'row'}, use_global_device_ids=true, to_apply=%region_8.0 | all-reduce | flops 160 | bytes 1280 | tf_op jit(solution)/shard_map/psum | solution.py:46
  491.4 0.9 multiply_add_fusion
  492.2 0.0 copy-start.1
  492.2 0.0 all-gather.8.cloned.1.call-update
  492.3 30.1 %all-gather.8.cloned.1.call-done = f32[4096,160]{0,1:T(8,128)} async-done(((f32[512,160]{0,1:T(8,128)}), f32[4096,160]{0,1:T(8,128)}) %all-gather.8.cloned.1.call-update) | async-done | bytes 2621456 | tf_op jit(solution)/shard_map/all_gather | solution.py:42
  522.4 13.2 %fusion = f32[160]{0:T(256)S(1)} fusion(f32[512,160]{0,1:T(8,128)} %multiply_add_fusion, f32[512,4096]{1,0:T(8,128)} %all-reduce.3.cloned.1.call-done, f32[4096,160]{0,1:T(8,128)} %all-gather.8.cloned.1.call-done), kind=kOutput, calls=%fused_computation.2 | convolution fusion | flops 4026695680 | bytes 11338368 | tf_op jit(solution)/shard_map/dot_general | solution.py:41
  535.7 13.1 %psum.39 = f32[160]{0:T(256)S(1)} all-reduce(f32[160]{0:T(256)S(1)} %fusion), channel_id=1, replica_groups=mesh['silo'=4,'row'=8] {'row'}, use_global_device_ids=true, to_apply=%region_10.0 | all-reduce | flops 160 | bytes 1280 | tf_op jit(solution)/shard_map/psum | solution.py:49
  548.7 0.0 copy-done.1
  548.8 0.1 add_bitcast_fusion
  548.9 10.9 %all_to_all.19 = f32[8,20,512]{2,1,0:T(8,128)S(1)} all-to-all(f32[8,20,512]{2,1,0:T(8,128)S(1)} %all_to_all.14), channel_id=1, replica_groups=mesh['silo'=4,'row'=8] {'row'}, dimensions={0} | all-to-all | bytes 655360 | tf_op jit(solution)/shard_map/all_to_all | solution.py:53
  559.8 0.2 copy.7
  560.0 1.0 copy.8
  (5 shorter events, 0.1 us)
Async XLA Ops:
  6.5 70.6 %all-gather.4.cloned.1.call-start = ((), (), s32[]{:S(2)}) async-start(), calls=%async_computation.2 | async-start | bytes 11796480 | tf_op jit(solution)/shard_map/all_gather | solution.py:34
  9.0 121.0 %reduce-scatter.2.cloned.1.call-start = ((), (), s32[]{:S(2)}) async-start(), calls=%async_computation.3 | async-start | bytes 1638400 | tf_op jit(solution)/shard_map/reduce_scatter | solution.py:38
  98.5 323.5 %all-reduce.3.cloned.1.call-start = ((), (), s32[]{:S(2)}) async-start(), calls=%async_computation.4 | async-start | bytes 16777216 | tf_op jit(solution)/shard_map/psum | solution.py:37
  110.1 342.7 %all-gather.6.cloned.1.call-start = ((), (), s32[]{:S(2)}) async-start(), calls=%async_computation.5 | async-start | bytes 2949120 | tf_op jit(solution)/shard_map/all_gather | solution.py:42
  130.0 349.2 %copy-start = (f32[512,160]{0,1:T(8,128)S(1)}, f32[512,160]{0,1:T(8,128)}, u32[]{:S(2)}) copy-start(f32[512,160]{0,1:T(8,128)} %reduce-scatter.2.cloned.1.call-done) | copy-start | bytes 983044
  130.0 392.4 %all-gather.8.cloned.1.call-start = ((), (), s32[]{:S(2)}) async-start(), calls=%async_computation.6 | async-start | bytes 2949120 | tf_op jit(solution)/shard_map/all_gather | solution.py:42
  492.2 56.5 %copy-start.1 = (f32[512,160]{0,1:T(8,128)S(1)}, f32[512,160]{0,1:T(8,128)}, u32[]{:S(2)}) copy-start(f32[512,160]{0,1:T(8,128)} %multiply_add_fusion) | copy-start | bytes 983044
Sparse Core Ops, SparseCore 0:
  9.2 67.8 all-gather.3
  98.6 31.3 reduce-scatter.1
  132.5 289.4 all-reduce.2
  423.8 28.9 all-gather.5
  492.4 29.9 all-gather.7
where the time goes:
time: 568 us
  waiting for transfers between devices  441 us (78%)
  blocking collectives  49 us (9%)
  matrix products  47.8 us (8%)
  between operations  13.2 us (2%)
  other arithmetic  12.8 us (2%)
    psum x1, waiting for transfers between devices, local(): operator = lax.psum(partial_op, 'silo')  292 us
    all_gather x1, waiting for transfers between devices, local(): lax.all_gather(silo_weights, 'row', axis=1, tiled=True).astype(jnp.float32)  68.1 us
    all_gather x2, waiting for transfers between devices, apply_cols(): lax.all_gather(direction, 'row', axis=0, tiled=True)  60.9 us
    dot_general x2, matrix products, apply_cols(): jnp.dot(operator, lax.all_gather(direction, 'row', axis=0, tiled=True), p...  26.5 us
    psum x2, blocking collectives, squares_cols(): return lax.psum(values, 'row')  25.1 us
    dot_general x1, matrix products, local(): jnp.einsum('srk,skc->rc', silo_grams, lax.all_gather(silo_weights, 'row',...  21.3 us
    reduce_scatter x1, waiting for transfers between devices, local(): lax.psum_scatter(partial_rhs, 'silo', scatter_dimension=1, tiled=True)  19.8 us
    psum x1, blocking collectives, curv_values(): return lax.psum(values, 'row')  13.1 us
  transfers between devices with their start and end apart: 5, of which 5 were waited for; matrix products, arithmetic and copies ran while one was open for 2% of the time, Pallas kernels for 0%

commit v1 on v0

v1 whole, which is shorter than its diff:
```python
import functools

import jax
import jax.numpy as jnp
from jax import lax
from jax.experimental import pallas as pl
from jax.experimental.pallas import tpu as pltpu
from jax.sharding import PartitionSpec as P


f32, bf16, f16 = jnp.float32, jnp.bfloat16, jnp.float16
CHUNKS = 1


def swap(value, axis, size, bit):
    return lax.ppermute(value, axis, [(i, i ^ bit) for i in range(size)])


def split(value):
    high = lax.reduce_precision(value, 8, 7)
    return high.astype(bf16), (value - high).astype(bf16)


def split_here(value):
    high = value.astype(bf16)
    return high, (value - high.astype(f32)).astype(bf16)


def nn(left, right):
    return lax.dot_general(left, right, (((1,), (0,)), ((), ())), preferred_element_type=f32)


def tile_of(rows):
    return 256 if rows % 256 == 0 else rows


def prepare_kernel(row_ref, gram_ref, high_ref, low_ref, sums_ref, diag_ref):
    block = pl.program_id(0)
    rows = gram_ref.shape[1]
    total = jnp.sum(gram_ref[...], axis=0)
    high, low = split_here(total.T)
    high_ref[...] = high
    low_ref[...] = low
    sizes = jnp.sum(jnp.abs(gram_ref[...]), axis=0)

    @pl.when(block == 0)
    def _():
        sums_ref[...] = jnp.zeros_like(sums_ref)

    sums_ref[...] += jnp.sum(sizes, axis=1, keepdims=True)

    @pl.when(block == row_ref[0])
    def _():
        here = lax.broadcasted_iota(jnp.int32, (rows, rows), 0)
        there = lax.broadcasted_iota(jnp.int32, (rows, rows), 1)
        diag_ref[...] = jnp.sum(jnp.where(here == there, total, 0.0), axis=1, keepdims=True)


def prepare(grams, row):
    silos, rows, width = grams.shape
    shape = jax.ShapeDtypeStruct
    return pl.pallas_call(
        prepare_kernel,
        grid_spec=pltpu.PrefetchScalarGridSpec(
            num_scalar_prefetch=1,
            grid=(width // rows,),
            in_specs=[pl.BlockSpec((silos, rows, rows), lambda k, row: (0, 0, k))],
            out_specs=[
                pl.BlockSpec((rows, rows), lambda k, row: (k, 0)),
                pl.BlockSpec((rows, rows), lambda k, row: (k, 0)),
                pl.BlockSpec((rows, 1), lambda k, row: (0, 0)),
                pl.BlockSpec((rows, 1), lambda k, row: (0, 0)),
            ],
        ),
        out_shape=[shape((width, rows), bf16), shape((width, rows), bf16), shape((rows, 1), f32), shape((rows, 1), f32)],
        cost_estimate=pl.CostEstimate(flops=400 * grams.size, bytes_accessed=6 * grams.size, transcendentals=0),
        name="prepare",
    )(row[None], grams)


def rhs_kernel(count, parts, last, where_ref, *refs):
    grams, weights, rest = refs[:count], refs[count : count * (1 + parts)], refs[count * (1 + parts) :]
    out_ref = rest[-1]
    total = rest[0][...] if len(rest) > 1 else None
    for k in range(count):
        tile = grams[k].shape[1]
        each = grams[k].shape[0] // parts
        for i in range(grams[k].shape[0]):
            both = jnp.concatenate(split_here(grams[k][i]), axis=0)
            term = nn(both, weights[k * parts + i // each][i % each])
            term = term[:tile] + term[tile:]
            total = term if total is None else total + term
    out_ref[...] = total.T if last else total


def rhs(pieces, grams, where, total, last):
    silos, rows, _ = grams.shape
    parts = len(pieces[0])
    depth, cols = pieces[0][0].shape[1:]
    tile = tile_of(rows)
    count = len(pieces)
    flat = [half for piece in pieces for half in piece]
    more = [] if total is None else [total]
    in_specs = [pl.BlockSpec((silos, tile, depth), functools.partial(lambda p, r, where: (0, r, where[p]), p)) for p in range(count)]
    in_specs += [pl.BlockSpec(half.shape, lambda r, where: (0, 0, 0)) for half in flat]
    in_specs += [pl.BlockSpec((tile, cols), lambda r, where: (r, 0)) for _ in more]
    return pl.pallas_call(
        functools.partial(rhs_kernel, count, parts, last),
        grid_spec=pltpu.PrefetchScalarGridSpec(
            num_scalar_prefetch=1,
            grid=(rows // tile,),
            in_specs=in_specs,
            out_specs=pl.BlockSpec((cols, tile), lambda r, where: (0, r)) if last else pl.BlockSpec((tile, cols), lambda r, where: (r, 0)),
        ),
        out_shape=jax.ShapeDtypeStruct((cols, rows) if last else (rows, cols), f32),
        cost_estimate=pl.CostEstimate(
            flops=8 * count * silos * rows * depth * cols, bytes_accessed=4 * count * silos * rows * depth, transcendentals=0
        ),
        name="rhs",
    )(where, *([grams] * count), *flat, *more)


def apply_kernel(shape, exact, where_ref, *refs):
    refs = list(refs)
    out_ref = refs.pop()
    values = [[[refs.pop(0)[...] for _ in range(groups)] for groups in shape] for _ in range(1 + exact)]
    high = [refs.pop(0) for _ in shape]
    low = [refs.pop(0) for _ in shape] if exact else None
    total = refs[0][...] if refs else None
    cols = out_ref.shape[0]
    for k in range(len(shape)):
        rows = [group for value in values for group in value[k]]
        term = nn(jnp.concatenate(rows, axis=0) if len(rows) > 1 else rows[0], high[k][...])
        if exact:
            first = values[0][k]
            more = nn(jnp.concatenate(first, axis=0) if len(first) > 1 else first[0], low[k][...])
            term = term[:cols] + (term[cols:] + more)
        total = term if total is None else total + term
    out_ref[...] = total


def apply(values, high, low, where, total):
    depth = values[0][0][0].shape[1]
    cols = sum(group.shape[0] for group in values[0][0])
    rows = high.shape[1]
    tile = tile_of(rows)
    shape = [len(piece) for piece in values[0]]
    count = len(shape)
    exact = len(values) > 1
    flat = [group for value in values for piece in value for group in piece]
    more = [] if total is None else [total]
    matrix = [pl.BlockSpec((depth, tile), functools.partial(lambda p, r, where: (where[p], r), p)) for p in range(count)]
    in_specs = [pl.BlockSpec(group.shape, lambda r, where: (0, 0)) for group in flat]
    in_specs += matrix * (1 + exact)
    in_specs += [pl.BlockSpec((cols, tile), lambda r, where: (0, r)) for _ in more]
    return pl.pallas_call(
        functools.partial(apply_kernel, shape, exact),
        grid_spec=pltpu.PrefetchScalarGridSpec(
            num_scalar_prefetch=1,
            grid=(rows // tile,),
            in_specs=in_specs,
            out_specs=pl.BlockSpec((cols, tile), lambda r, where: (0, r)),
        ),
        out_shape=jax.ShapeDtypeStruct((cols, rows), f32),
        cost_estimate=pl.CostEstimate(
            flops=(6 if exact else 2) * count * cols * depth * rows, bytes_accessed=6 * count * depth * rows, transcendentals=0
        ),
        name="apply",
    )(where, *flat, *([high] * count), *([low] * count if exact else []), *more)


def local(n_silo, n_row, silo_grams, silo_weights):
    return merge(n_silo, n_row, silo_grams, silo_weights)


def merge(n_silo, n_row, silo_grams, silo_weights):
    silos, rows, width = silo_grams.shape
    cols = silo_weights.shape[2]
    mine = cols // n_silo
    served = mine // n_row
    small = mine // CHUNKS
    silo, row = lax.axis_index("silo"), lax.axis_index("row")

    offsets = sorted(range(0, n_row, 2), key=lambda j: (bin(j).count("1"), j))
    final = offsets[-1]
    early = [j for j in offsets if j != final]

    def where(js):
        return row ^ jnp.array(js, jnp.int32)

    def hops(j):
        bits = [1 << k for k in range(1, n_row.bit_length()) if j >> k & 1]
        return bits[-1], bits[0]

    def gather_halves(halves):
        held = {0: list(halves)}
        for j in offsets[1:]:
            held[j] = []
            for p, hop in enumerate(hops(j)[: len(halves)]):
                held[j].append(swap(held[j ^ hop][p], "row", n_row, hop))
        return held

    def gather_rows(value):
        size = value.shape[0] // 2
        held = {0: [value]}

        def part(j, p):
            return held[j][p] if len(held[j]) == 2 else held[j][0][p * size : (p + 1) * size]

        for j in offsets[1:]:
            far, near = hops(j)
            if far == near:
                held[j] = [swap(value, "row", n_row, far)]
            else:
                held[j] = [swap(part(j ^ hop, p), "row", n_row, hop) for p, hop in enumerate((far, near))]
        return held

    def cross(value):
        return swap(value, "row", n_row, 1)

    def sum_silos(pieces):
        return sum((swap(pieces[j], "silo", n_silo, j) for j in range(1, n_silo)), pieces[0])

    def gather_silos(value):
        return jnp.concatenate([value] + [swap(value, "silo", n_silo, j) for j in range(1, n_silo)])

    half = silos // 2 if silos % 2 == 0 else silos
    held = gather_halves([silo_weights[i : i + half] for i in range(0, silos, half)])
    crossed = {j: [cross(x) for x in held[j]] for j in offsets}

    high, low, sums, diag = prepare(silo_grams, row)
    top = jnp.max(jnp.abs(silo_weights.astype(f32)))
    facts = jnp.stack([diag[:, 0], sums[:, 0], jnp.full((rows,), top)])
    others = [facts] + [swap(facts, "silo", n_silo, j) for j in range(1, n_silo)]
    diag = sum(o[0] for o in others)
    reach = jnp.max(sum(o[1] for o in others))
    top = functools.reduce(jnp.maximum, [o[2, 0] for o in others])
    lane = lax.broadcasted_iota(jnp.int32, (n_row, 128), 1)
    slot = lax.broadcasted_iota(jnp.int32, (n_row, 128), 0)
    entry = jnp.where(lane == 0, jnp.sum(diag * diag), jnp.where(lane == 1, jnp.sum(diag * diag * diag), jnp.where(lane == 2, reach, top)))
    table = lax.psum(jnp.where(slot == row, entry, 0.0), "row")
    shift = jnp.sum(table[:, 0]) / jnp.sum(table[:, 1])
    reach, top = jnp.max(table[:, 2]), jnp.max(table[:, 3])
    b_scale = 32768.0 / (reach * top)

    total = rhs([held[j] for j in early], silo_grams, where(early), None, False)
    total = rhs([crossed[j] for j in early], silo_grams, where([j ^ 1 for j in early]), total, False)
    total = rhs([held[final], crossed[final]], silo_grams, where([final, final ^ 1]), total, True)
    total = total.reshape(n_silo, CHUNKS, small, rows)
    b = [
        sum_silos([lax.dynamic_index_in_dim(total, silo ^ j, axis=0, keepdims=False)[c] for j in range(n_silo)])
        for c in range(CHUNKS)
    ]

    def multiply(values, low):
        crossed = [{j: [cross(x) for x in piece] for j, piece in held.items()} for held in values]
        both = [{**held, **{j ^ 1: piece for j, piece in other.items()}} for held, other in zip(values, crossed)]
        total = None
        for js in (early, [j ^ 1 for j in early], [final, final ^ 1]):
            total = apply([[x[j] for j in js] for x in both], high, low, where(js), total)
        return total

    def q_of(exact):
        sent = lax.reduce_precision(exact * b_scale, 5, 10)
        held = gather_rows(gather_silos(sent.astype(f16)))
        held = {j: [split(x.astype(f32)) for x in piece] for j, piece in held.items()}
        total = multiply([{j: [x[i] for x in piece] for j, piece in held.items()} for i in range(2)], low)
        lost = exact - sent / b_scale
        return sum_silos(list(total.reshape(n_silo, small, rows))) / b_scale + diag[None] * lost

    q = [q_of(x) for x in b]

    def curve_of(x, y):
        upper, lower = split(x - shift * y)
        upper, lower = gather_silos(upper), gather_silos(lower)
        total = multiply([gather_rows(upper)], None)
        return jnp.sum(total * (upper.astype(f32) + 2.0 * lower.astype(f32)), axis=1).reshape(n_silo, small)

    curved = jnp.concatenate([curve_of(x, y) for x, y in zip(b, q)], axis=1)
    curved = jnp.stack([lax.dynamic_index_in_dim(curved, silo ^ j, axis=0, keepdims=False) for j in range(n_silo)])
    curved = lax.all_to_all(curved.reshape(n_silo * n_row, served), ("silo", "row"), split_axis=0, concat_axis=0, tiled=True)
    vav = jnp.sum(curved, axis=0)

    both = jnp.stack([jnp.concatenate(b), jnp.concatenate(q)]).reshape(2, n_row, served, rows)
    both = lax.all_to_all(both, "row", split_axis=1, concat_axis=1, tiled=True)
    bt, qt = (jnp.swapaxes(x, 0, 1).reshape(served, width) for x in both)
    bb, bq, qq = (jnp.sum(x, axis=1) for x in (bt * bt, bt * qt, qt * qt))
    first = bb / bq
    next_norm = bb - 2.0 * first * bq + first * first * qq
    beta = next_norm / bb
    nu = first / shift
    mu = 1.0 + beta - nu
    curvature = mu * mu * bq + 2.0 * mu * nu * (bq - shift * qq) + nu * nu * vav
    second = next_norm / curvature
    return (first + second * (1.0 + beta))[:, None] * bt - (second * first)[:, None] * qt


def solution(mesh):
    placed = (P("silo", "row", None), P("silo", "row", None))
    body = functools.partial(local, mesh.shape["silo"], mesh.shape["row"])
    return jax.shard_map(body, mesh=mesh, in_specs=placed, out_specs=P(("silo", "row"), None), check_vma=False)
```

time: 568 us -> 320 us (0.56)
  waiting for transfers between devices: 441 us -> 112 us
  Pallas kernels: 0 us -> 78.1 us
  starting transfers between devices: 0.35 us -> 68.1 us
  matrix products: 47.8 us -> 0 us
  blocking collectives: 49 us -> 23.8 us
  local copies, waits for them, and re-layouts: 3.68 us -> 14.4 us
  between operations: 13.2 us -> 5.86 us
    psum x1 -> x0, waiting for transfers between devices: 292 us -> none  [local(): operator = lax.psum(partial_op, 'silo')]
    all_gather x3 -> x0, waiting for transfers between devices: 129 us -> none  [the longest x1 68.1 us: local(): lax.all_gather(silo_weights, 'row', axis=1, tiled=True).astype(jnp.float32)]
    ppermute x0 -> x55, waiting for transfers between devices: none -> 106 us  [swap(): return lax.ppermute(value, axis, [(i, i ^ bit) for i in range(size)])]
    pallas_call x0 -> x10, Pallas kernels: none -> 78.1 us  [the longest x6 36.5 us: apply(): pl.pallas_call(functools.partial(apply_kernel, shape, exact), grid_spec=p...]
    ppermute x0 -> x55, starting transfers between devices: none -> 60.4 us  [swap(): return lax.ppermute(value, axis, [(i, i ^ bit) for i in range(size)])]
    dot_general x3 -> x0, matrix products: 47.8 us -> none  [the longest x2 26.5 us: apply_cols(): jnp.dot(operator, lax.all_gather(direction, 'row', axis=0, tiled=True), p...]
    reduce_scatter x1 -> x0, waiting for transfers between devices: 19.8 us -> none  [local(): lax.psum_scatter(partial_rhs, 'silo', scatter_dimension=1, tiled=True)]
    psum x3 -> x1, blocking collectives: 38.2 us -> 23.8 us  [merge(): table = lax.psum(jnp.where(slot == row, entry, 0.0), 'row')]
  transfers between devices with their start and end apart: 5 -> 57, of which waited for: 5 -> 21; matrix products, arithmetic and copies ran while one was open for 2% -> 5% of each run, Pallas kernels for 0% -> 16%
where the time goes in v1:
time: 320 us
  waiting for transfers between devices  112 us (35%)
  Pallas kernels  78.1 us (24%)
  starting transfers between devices  68.1 us (21%)
  blocking collectives  23.8 us (7%)
  other arithmetic  17.5 us (5%)
  local copies, waits for them, and re-layouts  14.4 us (4%)
  between operations  5.86 us (2%)
    ppermute x55, waiting for transfers between devices, swap(): return lax.ppermute(value, axis, [(i, i ^ bit) for i in range(size)])  106 us
    ppermute x55, starting transfers between devices, swap(): return lax.ppermute(value, axis, [(i, i ^ bit) for i in range(size)])  60.4 us
    pallas_call x6, Pallas kernels, apply(): pl.pallas_call(functools.partial(apply_kernel, shape, exact), grid_spec=p...  36.5 us
    pallas_call x3, Pallas kernels, rhs(): pl.pallas_call(functools.partial(rhs_kernel, count, parts, last), grid_sp...  27.8 us
    psum x1, blocking collectives, merge(): table = lax.psum(jnp.where(slot == row, entry, 0.0), 'row')  23.8 us
    pallas_call x1, Pallas kernels, prepare(): pl.pallas_call(prepare_kernel, grid_spec=pltpu.PrefetchScalarGridSpec(num...  13.8 us
  transfers between devices with their start and end apart: 57, of which 21 were waited for; matrix products, arithmetic and copies ran while one was open for 5% of the time, Pallas kernels for 16%

profile of v1, /device:TPU:0, one launch (start us, length us, event | category | flops | bytes accessed | tf_op | source)
XLA Modules:
  0.0 319.6 jit_solution(7318374980386528286)
XLA Ops:
  0.0 13.8 %prepare.1 = (bf16[4096,512]{1,0:T(8,128)(2,1)}, bf16[4096,512]{1,0:T(8,128)(2,1)}, f32[512,1]{1,0:T(8,128)}, f32[512,1]{1,0:T(8,128)}) custom-call(s32[1]{0:T(128)} %bitcast.7.row_ref, f32[2,512,4096]{2,1,0:T(8,128)} %gram_ref.1), custom_call_target="tpu_custom_call" | custom-call | flops 1677721600 | bytes 25165824 | tf_op jit(solution)/shard_map/prepare/pallas_call | solution.py:62
  17.6 3.1 collective-permute-start.17
  20.6 2.6 collective-permute-start.18
  23.4 1.8 collective-permute-start
  25.2 1.5 collective-permute-start.2
  28.7 12.5 %collective-permute-done.refs_5_ = bf16[1,512,640]{2,1,0:T(8,128)(2,1)} collective-permute-done((bf16[1,512,640]{2,1,0:T(8,128)(2,1)S(1)}, bf16[1,512,640]{2,1,0:T(8,128)(2,1)}, u32[]{:S(2)}, u32[]{:S(2)}) %collective-permute-start) | collective-permute-done | bytes 655392 | tf_op jit(solution)/shard_map/ppermute | solution.py:16
  41.2 1.7 collective-permute-done.2.refs_8_
  49.5 5.1 %collective-permute-done.11.refs_7_ = bf16[1,512,640]{2,1,0:T(8,128)(2,1)} collective-permute-done((bf16[1,512,640]{2,1,0:T(8,128)(2,1)S(1)}, bf16[1,512,640]{2,1,0:T(8,128)(2,1)}, u32[]{:S(2)}, u32[]{:S(2)}) %collective-permute-start.11) | collective-permute-done | bytes 655392 | tf_op jit(solution)/shard_map/ppermute | solution.py:16
  54.6 1.7 collective-permute-start.1
  57.1 9.9 %rhs.7.refs_9_ = f32[512,640]{1,0:T(8,128)} custom-call(s32[3]{0:T(128)} %multiply_xor_fusion.where_ref, f32[2,512,4096]{2,1,0:T(8,128)} %gram_ref.1, f32[2,512,4096]{2,1,0:T(8,128)} %gram_ref.1, f32[2,512,4096]{2,1,0:T(8,128)} %gram_ref.1, bf16[1,512,640]{2,1,0:T(8,128)(2,1)} %copy-done.3, bf16[1,512,640]{2,1,0:T(8,128)(2,1)} %copy-done.2, ...), custom_call_target="tpu_custom_call" | custom-call | flops 8053063680 | bytes 6291456 | tf_op jit(solution)/shard_map/rhs/pallas_call | solution.py:107
  67.0 5.0 %collective-permute-done.1.refs_2_ = bf16[1,512,640]{2,1,0:T(8,128)(2,1)} collective-permute-done((bf16[1,512,640]{2,1,0:T(8,128)(2,1)}, bf16[1,512,640]{2,1,0:T(8,128)(2,1)}, u32[]{:S(2)}, u32[]{:S(2)}) %collective-permute-start.1) | collective-permute-done | bytes 655392 | tf_op jit(solution)/shard_map/ppermute | solution.py:16
  73.5 10.0 %rhs.8.refs_6_ = f32[512,640]{1,0:T(8,128)} custom-call(s32[3]{0:T(128)} %broadcast_xor_fusion.where_ref, f32[2,512,4096]{2,1,0:T(8,128)} %gram_ref.1, f32[2,512,4096]{2,1,0:T(8,128)} %gram_ref.1, f32[2,512,4096]{2,1,0:T(8,128)} %gram_ref.1, bf16[1,512,640]{2,1,0:T(8,128)(2,1)} %copy-done.16, bf16[1,512,640]{2,1,0:T(8,128)(2,1)} %copy-done.17, ...), custom_call_target="tpu_custom_call" | custom-call | flops 8053063680 | bytes 6291456 | tf_op jit(solution)/shard_map/rhs/pallas_call | solution.py:107
  85.2 7.9 %rhs.9 = f32[640,512]{1,0:T(8,128)} custom-call(s32[2]{0:T(128)} %broadcast_xor_fusion.1.where_ref, f32[2,512,4096]{2,1,0:T(8,128)} %gram_ref.1, f32[2,512,4096]{2,1,0:T(8,128)} %gram_ref.1, bf16[1,512,640]{2,1,0:T(8,128)(2,1)} %collective-permute-done.1.refs_2_, bf16[1,512,640]{2,1,0:T(8,128)(2,1)} %collective-permute-done.3.refs_3_, ...), custom_call_target="tpu_custom_call" | custom-call | flops 5368709120 | bytes 4194304 | tf_op jit(solution)/shard_map/rhs/pallas_call | solution.py:107
  95.0 3.5 %collective-permute-start.15 = (f32[160,512]{1,0:T(8,128)S(1)}, f32[160,512]{1,0:T(8,128)S(1)}, u32[]{:S(2)}, u32[]{:S(2)}) collective-permute-start(f32[160,512]{1,0:T(8,128)S(1)} %get-tuple-element.35), channel_id=1, source_target_pairs={{0,16},{8,24},{16,0},{24,8},{1,17},{9,25},{17,1},{25,9},{2,18},{10... | collective-permute-start | bytes 983048 | tf_op jit(solution)/shard_map/ppermute | solution.py:16
  100.1 23.8 %psum.7 = f32[8,128]{0,1:T(8,128)S(1)} all-reduce(f32[8,128]{0,1:T(8,128)S(1)} %select_select_fusion), channel_id=1, replica_groups=mesh['silo'=4,'row'=8] {'row'}, use_global_device_ids=true, to_apply=%region_4.5 | all-reduce | flops 1024 | bytes 8192 | tf_op jit(solution)/shard_map/psum | solution.py:241
  127.1 2.4 collective-permute-start.20
  129.6 1.7 collective-permute-start.21
  132.0 3.9 %collective-permute-done.20 = f16[160,512]{1,0:T(8,128)(2,1)S(1)} collective-permute-done((f16[160,512]{1,0:T(8,128)(2,1)S(1)}, f16[160,512]{1,0:T(8,128)(2,1)S(1)}, u32[]{:S(2)}, u32[]{:S(2)}) %collective-permute-start.20) | collective-permute-done | bytes 163872 | tf_op jit(solution)/shard_map/ppermute | solution.py:16
  135.9 8.7 %collective-permute-done.21 = f16[160,512]{1,0:T(8,128)(2,1)S(1)} collective-permute-done((f16[160,512]{1,0:T(8,128)(2,1)S(1)}, f16[160,512]{1,0:T(8,128)(2,1)S(1)}, u32[]{:S(2)}, u32[]{:S(2)}) %collective-permute-start.21) | collective-permute-done | bytes 163872 | tf_op jit(solution)/shard_map/ppermute | solution.py:16
  146.5 12.0 %collective-permute-done.23 = f16[640,512]{1,0:T(8,128)(2,1)S(1)} collective-permute-done((f16[640,512]{1,0:T(8,128)(2,1)S(1)}, f16[640,512]{1,0:T(8,128)(2,1)S(1)}, u32[]{:S(2)}, u32[]{:S(2)}) %collective-permute-start.23) | collective-permute-done | bytes 655392 | tf_op jit(solution)/shard_map/ppermute | solution.py:16
  159.8 3.1 collective-permute-start.26
  164.0 1.7 collective-permute-done.24
  165.7 3.5 %collective-permute-done.26 = f16[320,512]{1,0:T(8,128)(2,1)S(1)} collective-permute-done((f16[320,512]{1,0:T(8,128)(2,1)S(1)}, f16[320,512]{1,0:T(8,128)(2,1)S(1)}, u32[]{:S(2)}, u32[]{:S(2)}) %collective-permute-start.26) | collective-permute-done | bytes 327712 | tf_op jit(solution)/shard_map/ppermute | solution.py:16
  172.2 7.8 %apply.6.refs_12_ = f32[640,512]{1,0:T(8,128)} custom-call(s32[3]{0:T(128)} %multiply_xor_fusion.where_ref, bf16[640,512]{1,0:T(8,128)(2,1)} %copy-done.5, bf16[640,512]{1,0:T(8,128)(2,1)} %copy-done.7, bf16[640,512]{1,0:T(8,128)(2,1)} %copy-done.8, bf16[640,512]{1,0:T(8,128)(2,1)} %copy-done.4, bf16[640,512]{1,0:T(8,128)(2,1)} %copy-done.6, ...), custom_call_target="tpu_custom_call" | custom-call | flops 3019898880 | bytes 4718592 | tf_op jit(solution)/shard_map/apply/pallas_call | solution.py:156
  180.0 8.1 %apply.7.refs_12_ = f32[640,512]{1,0:T(8,128)} custom-call(s32[3]{0:T(128)} %broadcast_xor_fusion.where_ref, bf16[640,512]{1,0:T(8,128)(2,1)} %copy-done.26, bf16[640,512]{1,0:T(8,128)(2,1)} %copy-done.28, bf16[640,512]{1,0:T(8,128)(2,1)} %copy-done.29, bf16[640,512]{1,0:T(8,128)(2,1)} %copy-done.27, bf16[640,512]{1,0:T(8,128)(2,1)} %copy-done.30, ...), custom_call_target="tpu_custom_call" | custom-call | flops 3019898880 | bytes 4718592 | tf_op jit(solution)/shard_map/apply/pallas_call | solution.py:156
  188.1 6.4 %apply.8 = f32[640,512]{1,0:T(8,128)} custom-call(s32[2]{0:T(128)} %broadcast_xor_fusion.1.where_ref, bf16[320,512]{1,0:T(8,128)(2,1)} %copy-done.14, bf16[320,512]{1,0:T(8,128)(2,1)} %get-tuple-element.47.refs_1_, bf16[320,512]{1,0:T(8,128)(2,1)} %collective-permute-done.27.refs_2_, bf16[320,512]{1,0:T(8,128)(2,1)} %collective-permute-done.28.refs_3_, ...), custom_call_target="tpu_custom_call" | custom-call | flops 2013265920 | bytes 3145728 | tf_op jit(solution)/shard_map/apply/pallas_call | solution.py:156
  195.8 4.1 %collective-permute-start.37 = (f32[160,512]{1,0:T(8,128)S(1)}, f32[160,512]{1,0:T(8,128)S(1)}, u32[]{:S(2)}, u32[]{:S(2)}) collective-permute-start(f32[160,512]{1,0:T(8,128)S(1)} %get-tuple-element.30), channel_id=1, source_target_pairs={{0,8},{8,0},{16,24},{24,16},{1,9},{9,1},{17,25},{25,17},{2,10},{10... | collective-permute-start | bytes 983048 | tf_op jit(solution)/shard_map/ppermute | solution.py:16
  203.9 10.7 %collective-permute-done.37 = f32[160,512]{1,0:T(8,128)S(1)} collective-permute-done((f32[160,512]{1,0:T(8,128)S(1)}, f32[160,512]{1,0:T(8,128)S(1)}, u32[]{:S(2)}, u32[]{:S(2)}) %collective-permute-start.37) | collective-permute-done | bytes 327712 | tf_op jit(solution)/shard_map/ppermute | solution.py:16
  214.6 10.8 %collective-permute-done.38 = f32[160,512]{1,0:T(8,128)S(1)} collective-permute-done((f32[160,512]{1,0:T(8,128)S(1)}, f32[160,512]{1,0:T(8,128)S(1)}, u32[]{:S(2)}, u32[]{:S(2)}) %collective-permute-start.38) | collective-permute-done | bytes 327712 | tf_op jit(solution)/shard_map/ppermute | solution.py:16
  225.4 1.9 fusion.5
  227.4 6.7 %collective-permute-start.40 = (bf16[160,512]{1,0:T(8,128)(2,1)S(1)}, bf16[160,512]{1,0:T(8,128)(2,1)S(1)}, u32[]{:S(2)}, u32[]{:S(2)}) collective-permute-start(bf16[160,512]{1,0:T(8,128)(2,1)S(1)} %reduce-precision_convert_fusion.5), channel_id=1, source_target_pairs={{0,8},{8,0},{16,24},{24,16},{1,9},{9,1},{17,25},{25,17},{2,10},{10... | collective-permute-start | bytes 491528 | tf_op jit(solution)/shard_map/ppermute | solution.py:16
  236.8 2.8 collective-permute-done.40
  239.6 9.2 %collective-permute-done.41 = bf16[160,512]{1,0:T(8,128)(2,1)S(1)} collective-permute-done((bf16[160,512]{1,0:T(8,128)(2,1)S(1)}, bf16[160,512]{1,0:T(8,128)(2,1)S(1)}, u32[]{:S(2)}, u32[]{:S(2)}) %collective-permute-start.41) | collective-permute-done | bytes 163872 | tf_op jit(solution)/shard_map/ppermute | solution.py:16
  249.9 2.0 collective-permute-start.45
  253.3 3.8 %all-to-all-start = ((f32[2,8,20,512]{3,0,2,1:T(2,128)}), f32[2,8,20,512]{3,0,2,1:T(2,128)S(1)}, u32[]{:S(2)}, u32[]{:S(2)}) async-start(f32[2,8,20,512]{3,0,2,1:T(2,128)} %copy.49), calls=%async_computation | async-start | bytes 1310720 | tf_op jit(solution)/shard_map/all_to_all | solution.py:285
  257.3 7.3 %collective-permute-done.43.refs_1_ = bf16[640,512]{1,0:T(8,128)(2,1)S(1)} collective-permute-done((bf16[640,512]{1,0:T(8,128)(2,1)S(1)}, bf16[640,512]{1,0:T(8,128)(2,1)S(1)}, u32[]{:S(2)}, u32[]{:S(2)}) %collective-permute-start.43) | collective-permute-done | bytes 655392 | tf_op jit(solution)/shard_map/ppermute | solution.py:16
  266.0 2.3 collective-permute-start.44
  269.1 3.8 %collective-permute-start.46 = (bf16[320,512]{1,0:T(8,128)(2,1)}, bf16[320,512]{1,0:T(8,128)(2,1)}, u32[]{:S(2)}, u32[]{:S(2)}) collective-permute-start(bf16[320,512]{1,0:T(8,128)(2,1)} %slice.97), channel_id=1, source_target_pairs={{0,2},{1,3},{2,0},{3,1},{4,6},{5,7},{6,4},{7,5},{8,10},{9,11},{10,... | collective-permute-start | bytes 983048 | tf_op jit(solution)/shard_map/ppermute | solution.py:16
  273.4 4.2 %collective-permute-done.44.refs_0_ = bf16[320,512]{1,0:T(8,128)(2,1)} collective-permute-done((bf16[320,512]{1,0:T(8,128)(2,1)}, bf16[320,512]{1,0:T(8,128)(2,1)}, u32[]{:S(2)}, u32[]{:S(2)}) %collective-permute-start.44) | collective-permute-done | bytes 327712 | tf_op jit(solution)/shard_map/ppermute | solution.py:16
  277.6 3.6 %collective-permute-done.46.refs_1_ = bf16[320,512]{1,0:T(8,128)(2,1)} collective-permute-done((bf16[320,512]{1,0:T(8,128)(2,1)}, bf16[320,512]{1,0:T(8,128)(2,1)}, u32[]{:S(2)}, u32[]{:S(2)}) %collective-permute-start.46) | collective-permute-done | bytes 327712 | tf_op jit(solution)/shard_map/ppermute | solution.py:16
  281.6 4.4 %collective-permute-start.52 = (bf16[160,512]{1,0:T(8,128)(2,1)S(1)}, bf16[160,512]{1,0:T(8,128)(2,1)S(1)}, u32[]{:S(2)}, u32[]{:S(2)}) collective-permute-start(bf16[160,512]{1,0:T(8,128)(2,1)S(1)} %copy-done.19), channel_id=1, source_target_pairs={{0,8},{8,0},{16,24},{24,16},{1,9},{9,1},{17,25},{25,17},{2,10},{10... | collective-permute-start | bytes 491528 | tf_op jit(solution)/shard_map/ppermute | solution.py:16
  286.0 2.0 collective-permute-start.53
  289.4 4.8 %apply.9.refs_6_ = f32[640,512]{1,0:T(8,128)} custom-call(s32[3]{0:T(128)} %multiply_xor_fusion.where_ref, bf16[640,512]{1,0:T(8,128)(2,1)} %copy-done.1, bf16[640,512]{1,0:T(8,128)(2,1)} %copy-done.9, bf16[640,512]{1,0:T(8,128)(2,1)} %copy-done.10, bf16[4096,512]{1,0:T(8,128)(2,1)} %get-tuple-element.11.refs_6_.refs_7_.refs_8_.refs_9_.refs_3_.refs_4_.refs_5_, ...), custom_call_target="tpu_custom_call" | custom-call | flops 1006632960 | bytes 4718592 | tf_op jit(solution)/shard_map/apply/pallas_call | solution.py:156
  294.2 5.1 %apply.10.refs_6_ = f32[640,512]{1,0:T(8,128)} custom-call(s32[3]{0:T(128)} %broadcast_xor_fusion.where_ref, bf16[640,512]{1,0:T(8,128)(2,1)} %collective-permute-done.49.refs_0_, bf16[640,512]{1,0:T(8,128)(2,1)} %collective-permute-done.50.refs_1_, bf16[640,512]{1,0:T(8,128)(2,1)} %collective-permute-done.51.refs_2_, ...), custom_call_target="tpu_custom_call" | custom-call | flops 1006632960 | bytes 4718592 | tf_op jit(solution)/shard_map/apply/pallas_call | solution.py:156
  300.8 4.3 %apply.11 = f32[640,512]{1,0:T(8,128)} custom-call(s32[2]{0:T(128)} %broadcast_xor_fusion.1.where_ref, bf16[320,512]{1,0:T(8,128)(2,1)} %collective-permute-done.44.refs_0_, bf16[320,512]{1,0:T(8,128)(2,1)} %collective-permute-done.46.refs_1_, bf16[320,512]{1,0:T(8,128)(2,1)} %copy-done.33, bf16[320,512]{1,0:T(8,128)(2,1)} %copy-done.34, ...), custom_call_target="tpu_custom_call" | custom-call | flops 671088640 | bytes 3145728 | tf_op jit(solution)/shard_map/apply/pallas_call | solution.py:156
  305.2 1.6 multiply_reduce_fusion
  307.6 3.9 %all-to-all-start.1 = ((f32[32,1,20]{2,1,0:T(1,128)}), f32[32,1,20]{2,1,0:T(1,128)S(1)}, u32[]{:S(2)}, u32[]{:S(2)}) async-start(f32[32,1,20]{2,1,0:T(1,128)} %bitcast.24), calls=%async_computation.1 | async-start | bytes 32768 | tf_op jit(solution)/shard_map/all_to_all | solution.py:281
  312.4 6.3 %all-to-all-done.1 = f32[32,1,20]{2,1,0:T(1,128)S(1)} async-done(((f32[32,1,20]{2,1,0:T(1,128)}), f32[32,1,20]{2,1,0:T(1,128)S(1)}, u32[]{:S(2)}, u32[]{:S(2)}) %all-to-all-start.1) | async-done | bytes 2592 | tf_op jit(solution)/shard_map/all_to_all | solution.py:281
  (209 shorter events, 45.1 us)
Async XLA Ops:
  23.4 17.8 %collective-permute-start = (bf16[1,512,640]{2,1,0:T(8,128)(2,1)S(1)}, bf16[1,512,640]{2,1,0:T(8,128)(2,1)}, u32[]{:S(2)}, u32[]{:S(2)}) collective-permute-start(bf16[1,512,640]{2,1,0:T(8,128)(2,1)S(1)} %get-tuple-element.37.refs_3_), channel_id=1, source_target_pairs={{0,2},{1,3},{2,0},{3,1},{4,6},{5,7},{6,4},{7,5},{8,10},{9,11},{10,... | collective-permute-start | bytes 1966088 | tf_op jit(solution)/shard_map/ppermute | solution.py:16
  25.2 17.7 %collective-permute-start.2 = (bf16[1,512,640]{2,1,0:T(8,128)(2,1)S(1)}, bf16[1,512,640]{2,1,0:T(8,128)(2,1)}, u32[]{:S(2)}, u32[]{:S(2)}) collective-permute-start(bf16[1,512,640]{2,1,0:T(8,128)(2,1)S(1)} %get-tuple-element.36.refs_4_), channel_id=1, source_target_pairs={{0,4},{1,5},{2,6},{3,7},{4,0},{5,1},{6,2},{7,3},{8,12},{9,13},{10,... | collective-permute-start | bytes 1966088 | tf_op jit(solution)/shard_map/ppermute | solution.py:16
  27.7 26.8 %collective-permute-start.11 = (bf16[1,512,640]{2,1,0:T(8,128)(2,1)S(1)}, bf16[1,512,640]{2,1,0:T(8,128)(2,1)}, u32[]{:S(2)}, u32[]{:S(2)}) collective-permute-start(bf16[1,512,640]{2,1,0:T(8,128)(2,1)S(1)} %get-tuple-element.37.refs_3_), channel_id=1, source_target_pairs={{0,4},{1,5},{2,6},{3,7},{4,0},{5,1},{6,2},{7,3},{8,12},{9,13},{10,... | collective-permute-start | bytes 1966088 | tf_op jit(solution)/shard_map/ppermute | solution.py:16
  28.3 26.3 %collective-permute-start.9 = (bf16[1,512,640]{2,1,0:T(8,128)(2,1)S(1)}, bf16[1,512,640]{2,1,0:T(8,128)(2,1)}, u32[]{:S(2)}, u32[]{:S(2)}) collective-permute-start(bf16[1,512,640]{2,1,0:T(8,128)(2,1)S(1)} %get-tuple-element.36.refs_4_), channel_id=1, source_target_pairs={{0,2},{1,3},{2,0},{3,1},{4,6},{5,7},{6,4},{7,5},{8,10},{9,11},{10,... | collective-permute-start | bytes 1966088 | tf_op jit(solution)/shard_map/ppermute | solution.py:16
  28.7 27.6 %collective-permute-start.6 = (bf16[1,512,640]{2,1,0:T(8,128)(2,1)S(1)}, bf16[1,512,640]{2,1,0:T(8,128)(2,1)S(1)}, u32[]{:S(2)}, u32[]{:S(2)}) collective-permute-start(bf16[1,512,640]{2,1,0:T(8,128)(2,1)S(1)} %get-tuple-element.37.refs_3_), channel_id=1, source_target_pairs={{0,1},{1,0},{2,3},{3,2},{4,5},{5,4},{6,7},{7,6},{8,9},{9,8},{10,11... | collective-permute-start | bytes 1966088 | tf_op jit(solution)/shard_map/ppermute | solution.py:16
  41.2 15.5 %collective-permute-start.7 = (bf16[1,512,640]{2,1,0:T(8,128)(2,1)S(1)}, bf16[1,512,640]{2,1,0:T(8,128)(2,1)S(1)}, u32[]{:S(2)}, u32[]{:S(2)}) collective-permute-start(bf16[1,512,640]{2,1,0:T(8,128)(2,1)S(1)} %get-tuple-element.36.refs_4_), channel_id=1, source_target_pairs={{0,1},{1,0},{2,3},{3,2},{4,5},{5,4},{6,7},{7,6},{8,9},{9,8},{10,11... | collective-permute-start | bytes 1966088 | tf_op jit(solution)/shard_map/ppermute | solution.py:16
  42.9 13.8 %collective-permute-start.13 = (bf16[1,512,640]{2,1,0:T(8,128)(2,1)}, bf16[1,512,640]{2,1,0:T(8,128)(2,1)S(1)}, u32[]{:S(2)}, u32[]{:S(2)}) collective-permute-start(bf16[1,512,640]{2,1,0:T(8,128)(2,1)} %collective-permute-done.2.refs_8_), channel_id=1, source_target_pairs={{0,1},{1,0},{2,3},{3,2},{4,5},{5,4},{6,7},{7,6},{8,9},{9,8},{10,11... | collective-permute-start | bytes 1966088 | tf_op jit(solution)/shard_map/ppermute | solution.py:16
  54.5 18.9 %collective-permute-start.8 = (bf16[1,512,640]{2,1,0:T(8,128)(2,1)}, bf16[1,512,640]{2,1,0:T(8,128)(2,1)}, u32[]{:S(2)}, u32[]{:S(2)}) collective-permute-start(bf16[1,512,640]{2,1,0:T(8,128)(2,1)} %collective-permute-done.refs_5_), channel_id=1, source_target_pairs={{0,1},{1,0},{2,3},{3,2},{4,5},{5,4},{6,7},{7,6},{8,9},{9,8},{10,11... | collective-permute-start | bytes 1966088 | tf_op jit(solution)/shard_map/ppermute | solution.py:16
  54.6 17.5 %collective-permute-start.1 = (bf16[1,512,640]{2,1,0:T(8,128)(2,1)}, bf16[1,512,640]{2,1,0:T(8,128)(2,1)}, u32[]{:S(2)}, u32[]{:S(2)}) collective-permute-start(bf16[1,512,640]{2,1,0:T(8,128)(2,1)} %collective-permute-done.refs_5_), channel_id=1, source_target_pairs={{0,4},{1,5},{2,6},{3,7},{4,0},{5,1},{6,2},{7,3},{8,12},{9,13},{10,... | collective-permute-start | bytes 1966088 | tf_op jit(solution)/shard_map/ppermute | solution.py:16
  56.3 17.2 %collective-permute-start.3 = (bf16[1,512,640]{2,1,0:T(8,128)(2,1)}, bf16[1,512,640]{2,1,0:T(8,128)(2,1)}, u32[]{:S(2)}, u32[]{:S(2)}) collective-permute-start(bf16[1,512,640]{2,1,0:T(8,128)(2,1)} %collective-permute-done.2.refs_8_), channel_id=1, source_target_pairs={{0,2},{1,3},{2,0},{3,1},{4,6},{5,7},{6,4},{7,5},{8,10},{9,11},{10,... | collective-permute-start | bytes 1966088 | tf_op jit(solution)/shard_map/ppermute | solution.py:16
  56.6 16.8 %collective-permute-start.10 = (bf16[1,512,640]{2,1,0:T(8,128)(2,1)}, bf16[1,512,640]{2,1,0:T(8,128)(2,1)}, u32[]{:S(2)}, u32[]{:S(2)}) collective-permute-start(bf16[1,512,640]{2,1,0:T(8,128)(2,1)} %collective-permute-done.9.refs_6_), channel_id=1, source_target_pairs={{0,1},{1,0},{2,3},{3,2},{4,5},{5,4},{6,7},{7,6},{8,9},{9,8},{10,11... | collective-permute-start | bytes 1966088 | tf_op jit(solution)/shard_map/ppermute | solution.py:16
  56.6 16.8 %collective-permute-start.12 = (bf16[1,512,640]{2,1,0:T(8,128)(2,1)}, bf16[1,512,640]{2,1,0:T(8,128)(2,1)}, u32[]{:S(2)}, u32[]{:S(2)}) collective-permute-start(bf16[1,512,640]{2,1,0:T(8,128)(2,1)} %collective-permute-done.11.refs_7_), channel_id=1, source_target_pairs={{0,1},{1,0},{2,3},{3,2},{4,5},{5,4},{6,7},{7,6},{8,9},{9,8},{10,11... | collective-permute-start | bytes 1966088 | tf_op jit(solution)/shard_map/ppermute | solution.py:16
  72.0 11.5 %collective-permute-start.4 = (bf16[1,512,640]{2,1,0:T(8,128)(2,1)}, bf16[1,512,640]{2,1,0:T(8,128)(2,1)S(1)}, u32[]{:S(2)}, u32[]{:S(2)}) collective-permute-start(bf16[1,512,640]{2,1,0:T(8,128)(2,1)} %collective-permute-done.1.refs_2_), channel_id=1, source_target_pairs={{0,1},{1,0},{2,3},{3,2},{4,5},{5,4},{6,7},{7,6},{8,9},{9,8},{10,11... | collective-permute-start | bytes 1966088 | tf_op jit(solution)/shard_map/ppermute | solution.py:16
  94.4 31.5 %collective-permute-start.14 = (f32[160,512]{1,0:T(8,128)S(1)}, f32[160,512]{1,0:T(8,128)S(1)}, u32[]{:S(2)}, u32[]{:S(2)}) collective-permute-start(f32[160,512]{1,0:T(8,128)S(1)} %get-tuple-element.33), channel_id=1, source_target_pairs={{0,8},{8,0},{16,24},{24,16},{1,9},{9,1},{17,25},{25,17},{2,10},{10... | collective-permute-start | bytes 983048 | tf_op jit(solution)/shard_map/ppermute | solution.py:16
  95.0 30.9 %collective-permute-start.15 = (f32[160,512]{1,0:T(8,128)S(1)}, f32[160,512]{1,0:T(8,128)S(1)}, u32[]{:S(2)}, u32[]{:S(2)}) collective-permute-start(f32[160,512]{1,0:T(8,128)S(1)} %get-tuple-element.35), channel_id=1, source_target_pairs={{0,16},{8,24},{16,0},{24,8},{1,17},{9,25},{17,1},{25,9},{2,18},{10... | collective-permute-start | bytes 983048 | tf_op jit(solution)/shard_map/ppermute | solution.py:16
  98.5 27.4 %collective-permute-start.16 = (f32[160,512]{1,0:T(8,128)S(1)}, f32[160,512]{1,0:T(8,128)S(1)}, u32[]{:S(2)}, u32[]{:S(2)}) collective-permute-start(f32[160,512]{1,0:T(8,128)S(1)} %get-tuple-element.34), channel_id=1, source_target_pairs={{0,24},{8,16},{16,8},{24,0},{1,25},{9,17},{17,9},{25,1},{2,26},{10... | collective-permute-start | bytes 983048 | tf_op jit(solution)/shard_map/ppermute | solution.py:16
  129.6 15.0 %collective-permute-start.21 = (f16[160,512]{1,0:T(8,128)(2,1)S(1)}, f16[160,512]{1,0:T(8,128)(2,1)S(1)}, u32[]{:S(2)}, u32[]{:S(2)}) collective-permute-start(f16[160,512]{1,0:T(8,128)(2,1)S(1)} %get-tuple-element.28), channel_id=1, source_target_pairs={{0,16},{8,24},{16,0},{24,8},{1,17},{9,25},{17,1},{25,9},{2,18},{10... | collective-permute-start | bytes 491528 | tf_op jit(solution)/shard_map/ppermute | solution.py:16
  131.3 13.3 %collective-permute-start.22 = (f16[160,512]{1,0:T(8,128)(2,1)S(1)}, f16[160,512]{1,0:T(8,128)(2,1)S(1)}, u32[]{:S(2)}, u32[]{:S(2)}) collective-permute-start(f16[160,512]{1,0:T(8,128)(2,1)S(1)} %get-tuple-element.28), channel_id=1, source_target_pairs={{0,24},{8,16},{16,8},{24,0},{1,25},{9,17},{17,9},{25,1},{2,26},{10... | collective-permute-start | bytes 491528 | tf_op jit(solution)/shard_map/ppermute | solution.py:16
  144.8 13.7 %collective-permute-start.23 = (f16[640,512]{1,0:T(8,128)(2,1)S(1)}, f16[640,512]{1,0:T(8,128)(2,1)S(1)}, u32[]{:S(2)}, u32[]{:S(2)}) collective-permute-start(f16[640,512]{1,0:T(8,128)(2,1)S(1)} %pad_maximum_fusion.1), channel_id=1, source_target_pairs={{0,2},{1,3},{2,0},{3,1},{4,6},{5,7},{6,4},{7,5},{8,10},{9,11},{10,... | collective-permute-start | bytes 1966088 | tf_op jit(solution)/shard_map/ppermute | solution.py:16
  145.2 14.6 %collective-permute-start.25 = (f16[640,512]{1,0:T(8,128)(2,1)S(1)}, f16[640,512]{1,0:T(8,128)(2,1)S(1)}, u32[]{:S(2)}, u32[]{:S(2)}) collective-permute-start(f16[640,512]{1,0:T(8,128)(2,1)S(1)} %pad_maximum_fusion.1), channel_id=1, source_target_pairs={{0,4},{1,5},{2,6},{3,7},{4,0},{5,1},{6,2},{7,3},{8,12},{9,13},{10,... | collective-permute-start | bytes 1966088 | tf_op jit(solution)/shard_map/ppermute | solution.py:16
  145.9 18.0 %collective-permute-start.31 = (bf16[640,512]{1,0:T(8,128)(2,1)S(1)}, bf16[640,512]{1,0:T(8,128)(2,1)S(1)}, u32[]{:S(2)}, u32[]{:S(2)}) collective-permute-start(bf16[640,512]{1,0:T(8,128)(2,1)S(1)} %get-tuple-element.45.refs_0_), channel_id=1, source_target_pairs={{0,1},{1,0},{2,3},{3,2},{4,5},{5,4},{6,7},{7,6},{8,9},{9,8},{10,11... | collective-permute-start | bytes 1966088 | tf_op jit(solution)/shard_map/ppermute | solution.py:16
  146.0 24.3 %collective-permute-start.34 = (bf16[640,512]{1,0:T(8,128)(2,1)S(1)}, bf16[640,512]{1,0:T(8,128)(2,1)S(1)}, u32[]{:S(2)}, u32[]{:S(2)}) collective-permute-start(bf16[640,512]{1,0:T(8,128)(2,1)S(1)} %get-tuple-element.44.refs_3_), channel_id=1, source_target_pairs={{0,1},{1,0},{2,3},{3,2},{4,5},{5,4},{6,7},{7,6},{8,9},{9,8},{10,11... | collective-permute-start | bytes 1966088 | tf_op jit(solution)/shard_map/ppermute | solution.py:16
  158.9 11.9 %collective-permute-start.32 = (bf16[640,512]{1,0:T(8,128)(2,1)S(1)}, bf16[640,512]{1,0:T(8,128)(2,1)S(1)}, u32[]{:S(2)}, u32[]{:S(2)}) collective-permute-start(bf16[640,512]{1,0:T(8,128)(2,1)S(1)} %get-tuple-element.43.refs_1_), channel_id=1, source_target_pairs={{0,1},{1,0},{2,3},{3,2},{4,5},{5,4},{6,7},{7,6},{8,9},{9,8},{10,11... | collective-permute-start | bytes 1966088 | tf_op jit(solution)/shard_map/ppermute | solution.py:16
  169.2 10.8 %collective-permute-start.36 = (bf16[640,512]{1,0:T(8,128)(2,1)}, bf16[640,512]{1,0:T(8,128)(2,1)}, u32[]{:S(2)}, u32[]{:S(2)}) collective-permute-start(bf16[640,512]{1,0:T(8,128)(2,1)} %get-tuple-element.40.refs_5_), channel_id=1, source_target_pairs={{0,1},{1,0},{2,3},{3,2},{4,5},{5,4},{6,7},{7,6},{8,9},{9,8},{10,11... | collective-permute-start | bytes 1966088 | tf_op jit(solution)/shard_map/ppermute | solution.py:16
  170.3 17.8 %collective-permute-start.27 = (bf16[320,512]{1,0:T(8,128)(2,1)S(1)}, bf16[320,512]{1,0:T(8,128)(2,1)}, u32[]{:S(2)}, u32[]{:S(2)}) collective-permute-start(bf16[320,512]{1,0:T(8,128)(2,1)S(1)} %get-tuple-element.49.refs_0_), channel_id=1, source_target_pairs={{0,1},{1,0},{2,3},{3,2},{4,5},{5,4},{6,7},{7,6},{8,9},{9,8},{10,11... | collective-permute-start | bytes 983048 | tf_op jit(solution)/shard_map/ppermute | solution.py:16
  170.8 17.3 %collective-permute-start.28 = (bf16[320,512]{1,0:T(8,128)(2,1)}, bf16[320,512]{1,0:T(8,128)(2,1)}, u32[]{:S(2)}, u32[]{:S(2)}) collective-permute-start(bf16[320,512]{1,0:T(8,128)(2,1)} %get-tuple-element.47.refs_1_), channel_id=1, source_target_pairs={{0,1},{1,0},{2,3},{3,2},{4,5},{5,4},{6,7},{7,6},{8,9},{9,8},{10,11... | collective-permute-start | bytes 983048 | tf_op jit(solution)/shard_map/ppermute | solution.py:16
  170.9 17.2 %collective-permute-start.29 = (bf16[320,512]{1,0:T(8,128)(2,1)S(1)}, bf16[320,512]{1,0:T(8,128)(2,1)}, u32[]{:S(2)}, u32[]{:S(2)}) collective-permute-start(bf16[320,512]{1,0:T(8,128)(2,1)S(1)} %get-tuple-element.48.refs_4_), channel_id=1, source_target_pairs={{0,1},{1,0},{2,3},{3,2},{4,5},{5,4},{6,7},{7,6},{8,9},{9,8},{10,11... | collective-permute-start | bytes 983048 | tf_op jit(solution)/shard_map/ppermute | solution.py:16
  171.8 16.3 %collective-permute-start.30 = (bf16[320,512]{1,0:T(8,128)(2,1)S(1)}, bf16[320,512]{1,0:T(8,128)(2,1)}, u32[]{:S(2)}, u32[]{:S(2)}) collective-permute-start(bf16[320,512]{1,0:T(8,128)(2,1)S(1)} %get-tuple-element.46.refs_5_), channel_id=1, source_target_pairs={{0,1},{1,0},{2,3},{3,2},{4,5},{5,4},{6,7},{7,6},{8,9},{9,8},{10,11... | collective-permute-start | bytes 983048 | tf_op jit(solution)/shard_map/ppermute | solution.py:16
  195.8 18.8 %collective-permute-start.37 = (f32[160,512]{1,0:T(8,128)S(1)}, f32[160,512]{1,0:T(8,128)S(1)}, u32[]{:S(2)}, u32[]{:S(2)}) collective-permute-start(f32[160,512]{1,0:T(8,128)S(1)} %get-tuple-element.30), channel_id=1, source_target_pairs={{0,8},{8,0},{16,24},{24,16},{1,9},{9,1},{17,25},{25,17},{2,10},{10... | collective-permute-start | bytes 983048 | tf_op jit(solution)/shard_map/ppermute | solution.py:16
  199.9 25.5 %collective-permute-start.38 = (f32[160,512]{1,0:T(8,128)S(1)}, f32[160,512]{1,0:T(8,128)S(1)}, u32[]{:S(2)}, u32[]{:S(2)}) collective-permute-start(f32[160,512]{1,0:T(8,128)S(1)} %get-tuple-element.32), channel_id=1, source_target_pairs={{0,16},{8,24},{16,0},{24,8},{1,17},{9,25},{17,1},{25,9},{2,18},{10... | collective-permute-start | bytes 983048 | tf_op jit(solution)/shard_map/ppermute | solution.py:16
  201.2 24.2 %collective-permute-start.39 = (f32[160,512]{1,0:T(8,128)S(1)}, f32[160,512]{1,0:T(8,128)S(1)}, u32[]{:S(2)}, u32[]{:S(2)}) collective-permute-start(f32[160,512]{1,0:T(8,128)S(1)} %get-tuple-element.31), channel_id=1, source_target_pairs={{0,24},{8,16},{16,8},{24,0},{1,25},{9,17},{17,9},{25,1},{2,26},{10... | collective-permute-start | bytes 983048 | tf_op jit(solution)/shard_map/ppermute | solution.py:16
  227.4 12.2 %collective-permute-start.40 = (bf16[160,512]{1,0:T(8,128)(2,1)S(1)}, bf16[160,512]{1,0:T(8,128)(2,1)S(1)}, u32[]{:S(2)}, u32[]{:S(2)}) collective-permute-start(bf16[160,512]{1,0:T(8,128)(2,1)S(1)} %reduce-precision_convert_fusion.5), channel_id=1, source_target_pairs={{0,8},{8,0},{16,24},{24,16},{1,9},{9,1},{17,25},{25,17},{2,10},{10... | collective-permute-start | bytes 491528 | tf_op jit(solution)/shard_map/ppermute | solution.py:16
  234.1 14.7 %collective-permute-start.41 = (bf16[160,512]{1,0:T(8,128)(2,1)S(1)}, bf16[160,512]{1,0:T(8,128)(2,1)S(1)}, u32[]{:S(2)}, u32[]{:S(2)}) collective-permute-start(bf16[160,512]{1,0:T(8,128)(2,1)S(1)} %reduce-precision_convert_fusion.5), channel_id=1, source_target_pairs={{0,16},{8,24},{16,0},{24,8},{1,17},{9,25},{17,1},{25,9},{2,18},{10... | collective-permute-start | bytes 491528 | tf_op jit(solution)/shard_map/ppermute | solution.py:16
  235.4 13.4 %collective-permute-start.42 = (bf16[160,512]{1,0:T(8,128)(2,1)S(1)}, bf16[160,512]{1,0:T(8,128)(2,1)S(1)}, u32[]{:S(2)}, u32[]{:S(2)}) collective-permute-start(bf16[160,512]{1,0:T(8,128)(2,1)S(1)} %reduce-precision_convert_fusion.5), channel_id=1, source_target_pairs={{0,24},{8,16},{16,8},{24,0},{1,25},{9,17},{17,9},{25,1},{2,26},{10... | collective-permute-start | bytes 491528 | tf_op jit(solution)/shard_map/ppermute | solution.py:16
  249.5 15.1 %collective-permute-start.43 = (bf16[640,512]{1,0:T(8,128)(2,1)S(1)}, bf16[640,512]{1,0:T(8,128)(2,1)S(1)}, u32[]{:S(2)}, u32[]{:S(2)}) collective-permute-start(bf16[640,512]{1,0:T(8,128)(2,1)S(1)} %pad_maximum_fusion.2.refs_0_), channel_id=1, source_target_pairs={{0,2},{1,3},{2,0},{3,1},{4,6},{5,7},{6,4},{7,5},{8,10},{9,11},{10,... | collective-permute-start | bytes 1966088 | tf_op jit(solution)/shard_map/ppermute | solution.py:16
  249.9 15.4 %collective-permute-start.45 = (bf16[640,512]{1,0:T(8,128)(2,1)S(1)}, bf16[640,512]{1,0:T(8,128)(2,1)S(1)}, u32[]{:S(2)}, u32[]{:S(2)}) collective-permute-start(bf16[640,512]{1,0:T(8,128)(2,1)S(1)} %pad_maximum_fusion.2.refs_0_), channel_id=1, source_target_pairs={{0,4},{1,5},{2,6},{3,7},{4,0},{5,1},{6,2},{7,3},{8,12},{9,13},{10,... | collective-permute-start | bytes 1966088 | tf_op jit(solution)/shard_map/ppermute | solution.py:16
  253.3 19.5 %all-to-all-start = ((f32[2,8,20,512]{3,0,2,1:T(2,128)}), f32[2,8,20,512]{3,0,2,1:T(2,128)S(1)}, u32[]{:S(2)}, u32[]{:S(2)}) async-start(f32[2,8,20,512]{3,0,2,1:T(2,128)} %copy.49), calls=%async_computation | async-start | bytes 1310720 | tf_op jit(solution)/shard_map/all_to_all | solution.py:285
  257.1 24.4 %collective-permute-start.49 = (bf16[640,512]{1,0:T(8,128)(2,1)S(1)}, bf16[640,512]{1,0:T(8,128)(2,1)}, u32[]{:S(2)}, u32[]{:S(2)}) collective-permute-start(bf16[640,512]{1,0:T(8,128)(2,1)S(1)} %pad_maximum_fusion.2.refs_0_), channel_id=1, source_target_pairs={{0,1},{1,0},{2,3},{3,2},{4,5},{5,4},{6,7},{7,6},{8,9},{9,8},{10,11... | collective-permute-start | bytes 1966088 | tf_op jit(solution)/shard_map/ppermute | solution.py:16
  264.6 21.4 %collective-permute-start.50 = (bf16[640,512]{1,0:T(8,128)(2,1)S(1)}, bf16[640,512]{1,0:T(8,128)(2,1)}, u32[]{:S(2)}, u32[]{:S(2)}) collective-permute-start(bf16[640,512]{1,0:T(8,128)(2,1)S(1)} %collective-permute-done.43.refs_1_), channel_id=1, source_target_pairs={{0,1},{1,0},{2,3},{3,2},{4,5},{5,4},{6,7},{7,6},{8,9},{9,8},{10,11... | collective-permute-start | bytes 1966088 | tf_op jit(solution)/shard_map/ppermute | solution.py:16
  265.2 22.8 %collective-permute-start.51 = (bf16[640,512]{1,0:T(8,128)(2,1)S(1)}, bf16[640,512]{1,0:T(8,128)(2,1)}, u32[]{:S(2)}, u32[]{:S(2)}) collective-permute-start(bf16[640,512]{1,0:T(8,128)(2,1)S(1)} %collective-permute-done.45.refs_2_), channel_id=1, source_target_pairs={{0,1},{1,0},{2,3},{3,2},{4,5},{5,4},{6,7},{7,6},{8,9},{9,8},{10,11... | collective-permute-start | bytes 1966088 | tf_op jit(solution)/shard_map/ppermute | solution.py:16
  266.0 11.5 %collective-permute-start.44 = (bf16[320,512]{1,0:T(8,128)(2,1)}, bf16[320,512]{1,0:T(8,128)(2,1)}, u32[]{:S(2)}, u32[]{:S(2)}) collective-permute-start(bf16[320,512]{1,0:T(8,128)(2,1)} %slice.96), channel_id=1, source_target_pairs={{0,4},{1,5},{2,6},{3,7},{4,0},{5,1},{6,2},{7,3},{8,12},{9,13},{10,... | collective-permute-start | bytes 983048 | tf_op jit(solution)/shard_map/ppermute | solution.py:16
  269.1 12.1 %collective-permute-start.46 = (bf16[320,512]{1,0:T(8,128)(2,1)}, bf16[320,512]{1,0:T(8,128)(2,1)}, u32[]{:S(2)}, u32[]{:S(2)}) collective-permute-start(bf16[320,512]{1,0:T(8,128)(2,1)} %slice.97), channel_id=1, source_target_pairs={{0,2},{1,3},{2,0},{3,1},{4,6},{5,7},{6,4},{7,5},{8,10},{9,11},{10,... | collective-permute-start | bytes 983048 | tf_op jit(solution)/shard_map/ppermute | solution.py:16
  277.6 21.7 %collective-permute-start.47 = (bf16[320,512]{1,0:T(8,128)(2,1)}, bf16[320,512]{1,0:T(8,128)(2,1)S(1)}, u32[]{:S(2)}, u32[]{:S(2)}) collective-permute-start(bf16[320,512]{1,0:T(8,128)(2,1)} %collective-permute-done.44.refs_0_), channel_id=1, source_target_pairs={{0,1},{1,0},{2,3},{3,2},{4,5},{5,4},{6,7},{7,6},{8,9},{9,8},{10,11... | collective-permute-start | bytes 983048 | tf_op jit(solution)/shard_map/ppermute | solution.py:16
  281.2 18.1 %collective-permute-start.48 = (bf16[320,512]{1,0:T(8,128)(2,1)}, bf16[320,512]{1,0:T(8,128)(2,1)S(1)}, u32[]{:S(2)}, u32[]{:S(2)}) collective-permute-start(bf16[320,512]{1,0:T(8,128)(2,1)} %collective-permute-done.46.refs_1_), channel_id=1, source_target_pairs={{0,1},{1,0},{2,3},{3,2},{4,5},{5,4},{6,7},{7,6},{8,9},{9,8},{10,11... | collective-permute-start | bytes 983048 | tf_op jit(solution)/shard_map/ppermute | solution.py:16
  281.6 23.6 %collective-permute-start.52 = (bf16[160,512]{1,0:T(8,128)(2,1)S(1)}, bf16[160,512]{1,0:T(8,128)(2,1)S(1)}, u32[]{:S(2)}, u32[]{:S(2)}) collective-permute-start(bf16[160,512]{1,0:T(8,128)(2,1)S(1)} %copy-done.19), channel_id=1, source_target_pairs={{0,8},{8,0},{16,24},{24,16},{1,9},{9,1},{17,25},{25,17},{2,10},{10... | collective-permute-start | bytes 491528 | tf_op jit(solution)/shard_map/ppermute | solution.py:16
  286.0 19.1 %collective-permute-start.53 = (bf16[160,512]{1,0:T(8,128)(2,1)S(1)}, bf16[160,512]{1,0:T(8,128)(2,1)S(1)}, u32[]{:S(2)}, u32[]{:S(2)}) collective-permute-start(bf16[160,512]{1,0:T(8,128)(2,1)S(1)} %copy-done.19), channel_id=1, source_target_pairs={{0,16},{8,24},{16,0},{24,8},{1,17},{9,25},{17,1},{25,9},{2,18},{10... | collective-permute-start | bytes 491528 | tf_op jit(solution)/shard_map/ppermute | solution.py:16
  288.0 17.1 %collective-permute-start.54 = (bf16[160,512]{1,0:T(8,128)(2,1)S(1)}, bf16[160,512]{1,0:T(8,128)(2,1)S(1)}, u32[]{:S(2)}, u32[]{:S(2)}) collective-permute-start(bf16[160,512]{1,0:T(8,128)(2,1)S(1)} %copy-done.19), channel_id=1, source_target_pairs={{0,24},{8,16},{16,8},{24,0},{1,25},{9,17},{17,9},{25,1},{2,26},{10... | collective-permute-start | bytes 491528 | tf_op jit(solution)/shard_map/ppermute | solution.py:16
  307.6 11.0 %all-to-all-start.1 = ((f32[32,1,20]{2,1,0:T(1,128)}), f32[32,1,20]{2,1,0:T(1,128)S(1)}, u32[]{:S(2)}, u32[]{:S(2)}) async-start(f32[32,1,20]{2,1,0:T(1,128)} %bitcast.24), calls=%async_computation.1 | async-start | bytes 32768 | tf_op jit(solution)/shard_map/all_to_all | solution.py:281
  (46 other events, 433.1 us)

commit v2 on v1

v2 whole, which is shorter than its diff:
```python
import functools

import jax
import jax.numpy as jnp
from jax import lax
from jax.experimental import pallas as pl
from jax.experimental.pallas import tpu as pltpu
from jax.sharding import PartitionSpec as P


f32, bf16, f16 = jnp.float32, jnp.bfloat16, jnp.float16
CHUNKS = 1


def swap(value, axis, size, bit):
    return lax.ppermute(value, axis, [(i, i ^ bit) for i in range(size)])


def split(value):
    high = lax.reduce_precision(value, 8, 7)
    return high.astype(bf16), (value - high).astype(bf16)


def split_here(value):
    high = value.astype(bf16)
    return high, (value - high.astype(f32)).astype(bf16)


def nn(left, right):
    return lax.dot_general(left, right, (((1,), (0,)), ((), ())), preferred_element_type=f32)


def tile_of(rows):
    return 256 if rows % 256 == 0 else rows


def prepare_kernel(row_ref, gram_ref, weight_ref, high_ref, low_ref, facts_ref):
    block = pl.program_id(0)
    rows = gram_ref.shape[1]
    total = jnp.sum(gram_ref[...], axis=0).T
    high, low = split_here(total)
    high_ref[...] = high
    low_ref[...] = low
    sizes = jnp.sum(jnp.abs(gram_ref[...]), axis=0).astype(bf16)
    ones = jnp.ones((facts_ref.shape[0], rows), bf16)
    sums = lax.dot_general(ones, sizes, (((1,), (1,)), ((), ())), preferred_element_type=f32)
    place = lax.broadcasted_iota(jnp.int32, facts_ref.shape, 0)

    @pl.when(block == 0)
    def _():
        top = jnp.max(jnp.abs(weight_ref[...].astype(f32)))
        facts_ref[...] = jnp.where(place == 2, top / rows, 0.0)

    facts_ref[...] += jnp.where(place == 1, sums, 0.0)

    @pl.when(block == row_ref[0])
    def _():
        here = lax.broadcasted_iota(jnp.int32, (rows, rows), 0)
        there = lax.broadcasted_iota(jnp.int32, (rows, rows), 1)
        diag = jnp.sum(jnp.where(here == there, total, 0.0), axis=0, keepdims=True)
        facts_ref[...] += jnp.where(place == 0, diag, 0.0)


def prepare(grams, weights, row):
    silos, rows, width = grams.shape
    shape = jax.ShapeDtypeStruct
    return pl.pallas_call(
        prepare_kernel,
        grid_spec=pltpu.PrefetchScalarGridSpec(
            num_scalar_prefetch=1,
            grid=(width // rows,),
            in_specs=[
                pl.BlockSpec((silos, rows, rows), lambda k, row: (0, 0, k)),
                pl.BlockSpec(weights.shape, lambda k, row: (0, 0, 0)),
            ],
            out_specs=[
                pl.BlockSpec((rows, rows), lambda k, row: (k, 0)),
                pl.BlockSpec((rows, rows), lambda k, row: (k, 0)),
                pl.BlockSpec((8, rows), lambda k, row: (0, 0)),
            ],
        ),
        out_shape=[shape((width, rows), bf16), shape((width, rows), bf16), shape((8, rows), f32)],
        cost_estimate=pl.CostEstimate(flops=400 * grams.size, bytes_accessed=6 * grams.size, transcendentals=0),
        name="prepare",
    )(row[None], grams, weights)


def rhs_kernel(count, parts, last, where_ref, *refs):
    grams, weights, rest = refs[:count], refs[count : count * (1 + parts)], refs[count * (1 + parts) :]
    out_ref = rest[-1]
    total = rest[0][...] if len(rest) > 1 else None
    left, right = [], []
    for k in range(count):
        each = grams[k].shape[0] // parts
        for i in range(grams[k].shape[0]):
            left += split_here(grams[k][i])
            right += [weights[k * parts + i // each][i % each]] * 2
    term = nn(jnp.concatenate(left, axis=1), jnp.concatenate(right, axis=0))
    total = term if total is None else total + term
    out_ref[...] = total.T if last else total


def rhs(pieces, grams, where, total, last):
    silos, rows, _ = grams.shape
    parts = len(pieces[0])
    depth, cols = pieces[0][0].shape[1:]
    tile = tile_of(rows)
    count = len(pieces)
    flat = [half for piece in pieces for half in piece]
    more = [] if total is None else [total]
    in_specs = [pl.BlockSpec((silos, tile, depth), functools.partial(lambda p, r, where: (0, r, where[p]), p)) for p in range(count)]
    in_specs += [pl.BlockSpec(memory_space=pltpu.VMEM)] * len(flat)
    in_specs += [pl.BlockSpec((tile, cols), lambda r, where: (r, 0)) for _ in more]
    return pl.pallas_call(
        functools.partial(rhs_kernel, count, parts, last),
        grid_spec=pltpu.PrefetchScalarGridSpec(
            num_scalar_prefetch=1,
            grid=(rows // tile,),
            in_specs=in_specs,
            out_specs=pl.BlockSpec((cols, tile), lambda r, where: (0, r)) if last else pl.BlockSpec((tile, cols), lambda r, where: (r, 0)),
        ),
        out_shape=jax.ShapeDtypeStruct((cols, rows) if last else (rows, cols), f32),
        cost_estimate=pl.CostEstimate(
            flops=8 * count * silos * rows * depth * cols, bytes_accessed=4 * count * silos * rows * depth, transcendentals=0
        ),
        name="rhs",
    )(where, *([grams] * count), *flat, *more)


def apply_kernel(shape, exact, where_ref, *refs):
    refs = list(refs)
    out_ref = refs.pop()
    values = [[[refs.pop(0)[...] for _ in range(groups)] for groups in shape] for _ in range(1 + exact)]
    high = [refs.pop(0) for _ in shape]
    low = [refs.pop(0) for _ in shape] if exact else None
    total = refs[0][...] if refs else None
    left, right = [], []
    for k in range(len(shape)):
        rows = [value[k][0] if len(value[k]) == 1 else jnp.concatenate(value[k], axis=0) for value in values]
        left += rows + rows[: 1 if exact else 0]
        right += [high[k][...]] * len(rows) + ([low[k][...]] if exact else [])
    term = nn(left[0], right[0]) if len(left) == 1 else nn(jnp.concatenate(left, axis=1), jnp.concatenate(right, axis=0))
    out_ref[...] = term if total is None else total + term


def apply(values, high, low, where, total):
    depth = values[0][0][0].shape[1]
    cols = sum(group.shape[0] for group in values[0][0])
    rows = high.shape[1]
    tile = tile_of(rows)
    shape = [len(piece) for piece in values[0]]
    count = len(shape)
    exact = len(values) > 1
    flat = [group for value in values for piece in value for group in piece]
    more = [] if total is None else [total]
    matrix = [pl.BlockSpec((depth, tile), functools.partial(lambda p, r, where: (where[p], r), p)) for p in range(count)]
    in_specs = [pl.BlockSpec(memory_space=pltpu.VMEM)] * len(flat)
    in_specs += matrix * (1 + exact)
    in_specs += [pl.BlockSpec((cols, tile), lambda r, where: (0, r)) for _ in more]
    return pl.pallas_call(
        functools.partial(apply_kernel, shape, exact),
        grid_spec=pltpu.PrefetchScalarGridSpec(
            num_scalar_prefetch=1,
            grid=(rows // tile,),
            in_specs=in_specs,
            out_specs=pl.BlockSpec((cols, tile), lambda r, where: (0, r)),
        ),
        out_shape=jax.ShapeDtypeStruct((cols, rows), f32),
        cost_estimate=pl.CostEstimate(
            flops=(6 if exact else 2) * count * cols * depth * rows, bytes_accessed=6 * count * depth * rows, transcendentals=0
        ),
        name="apply",
    )(where, *flat, *([high] * count), *([low] * count if exact else []), *more)


def local(n_silo, n_row, silo_grams, silo_weights):
    return merge(n_silo, n_row, silo_grams, silo_weights)


def merge(n_silo, n_row, silo_grams, silo_weights):
    silos, rows, width = silo_grams.shape
    cols = silo_weights.shape[2]
    mine = cols // n_silo
    served = mine // n_row
    small = mine // CHUNKS
    silo, row = lax.axis_index("silo"), lax.axis_index("row")

    offsets = sorted(range(0, n_row, 2), key=lambda j: (bin(j).count("1"), j))
    levels = {}
    for j in offsets:
        levels.setdefault(bin(j).count("1"), []).extend([j, j ^ 1])
    levels = [levels[k] for k in sorted(levels)]

    def where(js):
        return row ^ jnp.array(js, jnp.int32)

    def hops(j):
        bits = [1 << k for k in range(1, n_row.bit_length()) if j >> k & 1]
        return bits[-1], bits[0]

    def gather_halves(halves):
        held = {0: list(halves)}
        for j in offsets[1:]:
            held[j] = []
            for p, hop in enumerate(hops(j)[: len(halves)]):
                held[j].append(swap(held[j ^ hop][p], "row", n_row, hop))
        return held

    def cross(value):
        return swap(value, "row", n_row, 1)

    def sum_silos(pieces):
        return sum((swap(pieces[j], "silo", n_silo, j) for j in range(1, n_silo)), pieces[0])

    def gather_silos(value):
        held = [value]
        for j in range(1, n_silo):
            held.append(swap(value, "silo", n_silo, j))
        return [jnp.concatenate(held[: n_silo // 2]), jnp.concatenate(held[n_silo // 2 :])]

    half = silos // 2 if silos % 2 == 0 else silos
    held = gather_halves([silo_weights[i : i + half] for i in range(0, silos, half)])
    crossed = {j: [cross(x) for x in held[j]] for j in offsets}

    high, low, facts = prepare(silo_grams, silo_weights, row)
    others = [facts]
    for j in range(1, n_silo):
        others.append(swap(facts, "silo", n_silo, j))
    facts = sum(others)
    diag = facts[0]
    place = lax.broadcasted_iota(jnp.int32, facts.shape, 0)
    facts = jnp.where(place == 0, diag * diag, jnp.where(place == 3, diag * diag * diag, facts))
    facts = jnp.sum(facts, axis=1)
    held.update({j ^ 1: piece for j, piece in crossed.items()})
    total = None
    for k, js in enumerate(levels):
        total = rhs([held[j] for j in js], silo_grams, where(js), total, js is levels[-1])
        if k == 0:
            total, diag, facts = lax.optimization_barrier((total, diag, facts))
    slot = lax.broadcasted_iota(jnp.int32, (n_row, 8), 0)
    table = lax.psum(jnp.where(slot == row, facts[None], 0.0), "row")
    shift = jnp.sum(table[:, 0]) / jnp.sum(table[:, 3])
    reach = 1.01 * jnp.max(table[:, 1])
    top = jnp.max(table[:, 2])
    b_scale = 32768.0 / (reach * top)

    total = total.reshape(n_silo, CHUNKS, small, rows)
    b = [
        sum_silos([lax.dynamic_index_in_dim(total, silo ^ j, axis=0, keepdims=False)[c] for j in range(n_silo)])
        for c in range(CHUNKS)
    ]

    def multiply(values, low):
        crossed = [{j: [cross(x) for x in piece] for j, piece in held.items()} for held in values]
        both = [{**held, **{j ^ 1: piece for j, piece in other.items()}} for held, other in zip(values, crossed)]
        total = None
        for js in levels:
            before = total
            total = apply([[x[j] for j in js] for x in both], high, low, where(js), total)
        return before, total

    def q_of(exact):
        sent = lax.reduce_precision(exact * b_scale, 5, 10)
        held = gather_halves(gather_silos(sent.astype(f16)))
        for piece in held.values():
            for p, x in enumerate(piece):
                piece[p] = split(x.astype(f32))
        _, total = multiply([{j: [x[i] for x in piece] for j, piece in held.items()} for i in range(2)], low)
        lost = exact - sent / b_scale
        return sum_silos(list(total.reshape(n_silo, small, rows))) / b_scale + diag[None] * lost

    q = [q_of(x) for x in b]

    def curve_of(x, y):
        upper, lower = split(x - shift * y)
        upper, lower = gather_silos(upper), gather_silos(lower)
        held = gather_halves(upper)
        before = [held[j][0][:8, :128] for j in offsets if bin(j).count("1") == 1]
        _, total = multiply([held], None)
        rounded = jnp.concatenate(upper).astype(f32) + 2.0 * jnp.concatenate(lower).astype(f32)
        return before, jnp.sum(total * rounded, axis=1).reshape(n_silo, small)

    curves = [curve_of(x, y) for x, y in zip(b, q)]
    curved = jnp.concatenate([curve for _, curve in curves], axis=1)
    curved = jnp.stack([lax.dynamic_index_in_dim(curved, silo ^ j, axis=0, keepdims=False) for j in range(n_silo)])
    both = jnp.stack([jnp.concatenate(b), jnp.concatenate(q)]).reshape(2, n_row, served, rows)
    both, _ = lax.optimization_barrier((both, curves[-1][0]))
    both = lax.all_to_all(both, "row", split_axis=1, concat_axis=1, tiled=True)
    both, curved = lax.optimization_barrier((both, curved))
    curved = lax.all_to_all(curved.reshape(n_silo * n_row, served), ("silo", "row"), split_axis=0, concat_axis=0, tiled=True)
    vav = jnp.sum(curved, axis=0)
    bt, qt = (jnp.swapaxes(x, 0, 1).reshape(served, width) for x in both)
    bb, bq, qq = (jnp.sum(x, axis=1) for x in (bt * bt, bt * qt, qt * qt))
    first = bb / bq
    next_norm = bb - 2.0 * first * bq + first * first * qq
    beta = next_norm / bb
    nu = first / shift
    mu = 1.0 + beta - nu
    curvature = mu * mu * bq + 2.0 * mu * nu * (bq - shift * qq) + nu * nu * vav
    second = next_norm / curvature
    return (first + second * (1.0 + beta))[:, None] * bt - (second * first)[:, None] * qt


def solution(mesh):
    placed = (P("silo", "row", None), P("silo", "row", None))
    body = functools.partial(local, mesh.shape["silo"], mesh.shape["row"])
    return jax.shard_map(body, mesh=mesh, in_specs=placed, out_specs=P(("silo", "row"), None), check_vma=False)
```

time: 320 us -> 315 us (0.984)
  blocking collectives: 23.8 us -> 13.2 us
  starting transfers between devices: 68.1 us -> 74.8 us
  waiting for transfers between devices: 112 us -> 118 us
    psum x1, blocking collectives: 23.8 us -> 13.2 us  [merge(): table = lax.psum(jnp.where(slot == row, facts[None], 0.0), 'row')]
    ppermute x55 -> x68, waiting for transfers between devices: 106 us -> 111 us  [swap(): return lax.ppermute(value, axis, [(i, i ^ bit) for i in range(size)])]
    ppermute x55 -> x68, starting transfers between devices: 60.4 us -> 64.7 us  [swap(): return lax.ppermute(value, axis, [(i, i ^ bit) for i in range(size)])]
    slice x7 -> x1, local copies, waits for them, and re-layouts: 3.22 us -> 0.01 us  [merge(): diag = facts[0]]
    convert_element_type x7 -> x10, other arithmetic: 4.55 us -> 7.45 us  [split(): return (high.astype(bf16), (value - high).astype(bf16))]
  transfers between devices with their start and end apart: 57 -> 70, of which waited for: 21 -> 23; matrix products, arithmetic and copies ran while one was open for 5% -> 4% of each run, Pallas kernels for 16% -> 20%
where the time goes in v2:
time: 315 us; the launch traced here: 314 us
  waiting for transfers between devices  118 us (37%)
  Pallas kernels  77 us (24%)
  starting transfers between devices  74.8 us (24%)
  other arithmetic  15 us (5%)
  blocking collectives  13.2 us (4%)
  local copies, waits for them, and re-layouts  12.8 us (4%)
  between operations  3.48 us (1%)
    ppermute x68, waiting for transfers between devices, swap(): return lax.ppermute(value, axis, [(i, i ^ bit) for i in range(size)])  111 us
    ppermute x68, starting transfers between devices, swap(): return lax.ppermute(value, axis, [(i, i ^ bit) for i in range(size)])  64.7 us
    pallas_call x6, Pallas kernels, apply(): pl.pallas_call(functools.partial(apply_kernel, shape, exact), grid_spec=p...  36.5 us
    pallas_call x3, Pallas kernels, rhs(): pl.pallas_call(functools.partial(rhs_kernel, count, parts, last), grid_sp...  27.8 us
    psum x1, blocking collectives, merge(): table = lax.psum(jnp.where(slot == row, facts[None], 0.0), 'row')  13.2 us
    pallas_call x1, Pallas kernels, prepare(): pl.pallas_call(prepare_kernel, grid_spec=pltpu.PrefetchScalarGridSpec(num...  12.8 us
    convert_element_type x10, other arithmetic, split(): return (high.astype(bf16), (value - high).astype(bf16))  7.45 us
    all_to_all x1, waiting for transfers between devices, merge(): lax.all_to_all(curved.reshape(n_silo * n_row, served), ('silo', 'row'), s...  6.53 us
  transfers between devices with their start and end apart: 70, of which 23 were waited for; matrix products, arithmetic and copies ran while one was open for 4% of the time, Pallas kernels for 20%

profile of v2, /device:TPU:0, one launch (start us, length us, event | category | flops | bytes accessed | tf_op | source)
XLA Modules:
  0.0 314.2 jit_solution(553930781200524671)
XLA Ops:
  2.0 2.6 collective-permute-start.2
  4.6 12.8 %prepare.1 = (bf16[4096,512]{1,0:T(8,128)(2,1)}, bf16[4096,512]{1,0:T(8,128)(2,1)}, f32[8,512]{1,0:T(8,128)}) custom-call(s32[1]{0:T(128)} %bitcast.row_ref, f32[2,512,4096]{2,1,0:T(8,128)} %refs_1_.5, bf16[2,512,640]{2,1,0:T(8,128)(2,1)} %weight_ref.1), custom_call_target="tpu_custom_call" | custom-call | flops 1677721600 | bytes 25165824 | tf_op jit(solution)/shard_map/prepare/pallas_call | solution.py:67
  17.3 1.6 collective-permute-start.14
  18.9 2.6 collective-permute-start.15
  22.4 1.5 collective-permute-done.15
  23.9 1.5 collective-permute-start
  25.4 1.9 collective-permute-done.16
  31.0 10.5 %collective-permute-done.refs_4_ = bf16[1,512,640]{2,1,0:T(8,128)(2,1)S(1)} collective-permute-done((bf16[1,512,640]{2,1,0:T(8,128)(2,1)S(1)}, bf16[1,512,640]{2,1,0:T(8,128)(2,1)S(1)}, u32[]{:S(2)}, u32[]{:S(2)}) %collective-permute-start) | collective-permute-done | bytes 655392 | tf_op jit(solution)/shard_map/ppermute | solution.py:16
  42.3 1.5 collective-permute-start.3
  43.8 11.9 %collective-permute-done.6.refs_5_ = bf16[1,512,640]{2,1,0:T(8,128)(2,1)} collective-permute-done((bf16[1,512,640]{2,1,0:T(8,128)(2,1)S(1)}, bf16[1,512,640]{2,1,0:T(8,128)(2,1)}, u32[]{:S(2)}, u32[]{:S(2)}) %collective-permute-start.6) | collective-permute-done | bytes 655392 | tf_op jit(solution)/shard_map/ppermute | solution.py:16
  57.2 7.5 %rhs.3.refs_12_ = f32[512,640]{1,0:T(8,128)} custom-call(s32[2]{0:T(128)} %iota_xor_fusion.where_ref, f32[2,512,4096]{2,1,0:T(8,128)} %refs_1_.5, f32[2,512,4096]{2,1,0:T(8,128)} %refs_1_.5, bf16[1,512,640]{2,1,0:T(8,128)(2,1)} %copy-done.1, bf16[1,512,640]{2,1,0:T(8,128)(2,1)} %copy-done, bf16[1,512,640]{2,1,0:T(8,128)(2,1)} %collective-permute-done.12.refs_4_, ...), custom_call_target="tpu_custom_call" | custom-call | flops 5368709120 | bytes 4194304 | tf_op jit(solution)/shard_map/rhs/pallas_call | solution.py:114
  64.8 2.9 collective-permute-done.3.refs_3_
  69.5 12.4 %rhs.4.refs_6_ = f32[512,640]{1,0:T(8,128)} custom-call(s32[4]{0:T(128)} %broadcast_xor_fusion.where_ref, f32[2,512,4096]{2,1,0:T(8,128)} %refs_1_.5, f32[2,512,4096]{2,1,0:T(8,128)} %refs_1_.5, f32[2,512,4096]{2,1,0:T(8,128)} %refs_1_.5, f32[2,512,4096]{2,1,0:T(8,128)} %refs_1_.5, bf16[1,512,640]{2,1,0:T(8,128)(2,1)} %copy-done.21, ...), custom_call_target="tpu_custom_call" | custom-call | flops 10737418240 | bytes 8388608 | tf_op jit(solution)/shard_map/rhs/pallas_call | solution.py:114
  82.7 7.9 %rhs.5 = f32[640,512]{1,0:T(8,128)} custom-call(s32[2]{0:T(128)} %broadcast_xor_fusion.1.where_ref, f32[2,512,4096]{2,1,0:T(8,128)} %refs_1_.5, f32[2,512,4096]{2,1,0:T(8,128)} %refs_1_.5, bf16[1,512,640]{2,1,0:T(8,128)(2,1)} %collective-permute-done.1.refs_2_, bf16[1,512,640]{2,1,0:T(8,128)(2,1)} %collective-permute-done.3.refs_3_, ...), custom_call_target="tpu_custom_call" | custom-call | flops 5368709120 | bytes 4194304 | tf_op jit(solution)/shard_map/rhs/pallas_call | solution.py:114
  92.6 3.5 %collective-permute-start.18 = (f32[160,512]{1,0:T(8,128)S(1)}, f32[160,512]{1,0:T(8,128)S(1)}, u32[]{:S(2)}, u32[]{:S(2)}) collective-permute-start(f32[160,512]{1,0:T(8,128)S(1)} %get-tuple-element.41), channel_id=1, source_target_pairs={{0,16},{8,24},{16,0},{24,8},{1,17},{9,25},{17,1},{25,9},{2,18},{10... | collective-permute-start | bytes 983048 | tf_op jit(solution)/shard_map/ppermute | solution.py:16
  96.3 13.2 %psum.7 = f32[8,8]{0,1:T(8,128)S(1)} all-reduce(f32[8,8]{0,1:T(8,128)S(1)} %broadcast_select_fusion), channel_id=1, replica_groups=mesh['silo'=4,'row'=8] {'row'}, use_global_device_ids=true, to_apply=%region_1.2 | all-reduce | flops 64 | bytes 512 | tf_op jit(solution)/shard_map/psum | solution.py:241
  111.5 7.2 %collective-permute-done.18 = f32[160,512]{1,0:T(8,128)S(1)} collective-permute-done((f32[160,512]{1,0:T(8,128)S(1)}, f32[160,512]{1,0:T(8,128)S(1)}, u32[]{:S(2)}, u32[]{:S(2)}) %collective-permute-start.18) | collective-permute-done | bytes 327712 | tf_op jit(solution)/shard_map/ppermute | solution.py:16
  119.9 8.2 %collective-permute-start.23 = (f16[160,512]{1,0:T(8,128)(2,1)S(1)}, f16[160,512]{1,0:T(8,128)(2,1)S(1)}, u32[]{:S(2)}, u32[]{:S(2)}) collective-permute-start(f16[160,512]{1,0:T(8,128)(2,1)S(1)} %get-tuple-element.34), channel_id=1, source_target_pairs={{0,16},{8,24},{16,0},{24,8},{1,17},{9,25},{17,1},{25,9},{2,18},{10... | collective-permute-start | bytes 491528 | tf_op jit(solution)/shard_map/ppermute | solution.py:16
  129.4 10.7 %collective-permute-done.23 = f16[160,512]{1,0:T(8,128)(2,1)S(1)} collective-permute-done((f16[160,512]{1,0:T(8,128)(2,1)S(1)}, f16[160,512]{1,0:T(8,128)(2,1)S(1)}, u32[]{:S(2)}, u32[]{:S(2)}) %collective-permute-start.23) | collective-permute-done | bytes 163872 | tf_op jit(solution)/shard_map/ppermute | solution.py:16
  140.2 1.5 collective-permute-start.31
  143.0 1.5 collective-permute-start.34
  144.9 6.0 %collective-permute-done.31 = f16[320,512]{1,0:T(8,128)(2,1)S(1)} collective-permute-done((f16[320,512]{1,0:T(8,128)(2,1)S(1)}, f16[320,512]{1,0:T(8,128)(2,1)S(1)}, u32[]{:S(2)}, u32[]{:S(2)}) %collective-permute-start.31) | collective-permute-done | bytes 327712 | tf_op jit(solution)/shard_map/ppermute | solution.py:16
  152.5 2.6 collective-permute-done.21
  158.7 1.5 collective-permute-start.26
  160.6 6.1 %apply.6.refs_24_ = f32[640,512]{1,0:T(8,128)} custom-call(s32[2]{0:T(128)} %iota_xor_fusion.where_ref, bf16[320,512]{1,0:T(8,128)(2,1)} %copy-done.14, bf16[320,512]{1,0:T(8,128)(2,1)} %copy-done.12, bf16[320,512]{1,0:T(8,128)(2,1)} %copy-done.38, bf16[320,512]{1,0:T(8,128)(2,1)} %copy-done.41, bf16[320,512]{1,0:T(8,128)(2,1)} %copy-done.13, ...), custom_call_target="tpu_custom_call" | custom-call | flops 2013265920 | bytes 3145728 | tf_op jit(solution)/shard_map/apply/pallas_call | solution.py:160
  174.2 9.7 %apply.7.refs_12_ = f32[640,512]{1,0:T(8,128)} custom-call(s32[4]{0:T(128)} %broadcast_xor_fusion.where_ref, bf16[320,512]{1,0:T(8,128)(2,1)} %copy-done.7, bf16[320,512]{1,0:T(8,128)(2,1)} %copy-done.3, bf16[320,512]{1,0:T(8,128)(2,1)} %copy-done.30, bf16[320,512]{1,0:T(8,128)(2,1)} %collective-permute-done.33.refs_3_, bf16[320,512]{1,0:T(8,128)(2,1)} %copy-done.9, ...), custom_call_target="tpu_custom_call" | custom-call | flops 4026531840 | bytes 6291456 | tf_op jit(solution)/shard_map/apply/pallas_call | solution.py:160
  185.6 6.4 %apply.8 = f32[640,512]{1,0:T(8,128)} custom-call(s32[2]{0:T(128)} %broadcast_xor_fusion.1.where_ref, bf16[320,512]{1,0:T(8,128)(2,1)} %copy-done.18, bf16[320,512]{1,0:T(8,128)(2,1)} %copy-done.16, bf16[320,512]{1,0:T(8,128)(2,1)} %collective-permute-done.27.refs_2_, bf16[320,512]{1,0:T(8,128)(2,1)} %copy-done.40, bf16[320,512]{1,0:T(8,128)(2,1)} %copy-done.17, ...), custom_call_target="tpu_custom_call" | custom-call | flops 2013265920 | bytes 3145728 | tf_op jit(solution)/shard_map/apply/pallas_call | solution.py:160
  193.2 4.1 %collective-permute-start.45 = (f32[160,512]{1,0:T(8,128)S(1)}, f32[160,512]{1,0:T(8,128)S(1)}, u32[]{:S(2)}, u32[]{:S(2)}) collective-permute-start(f32[160,512]{1,0:T(8,128)S(1)} %get-tuple-element.36), channel_id=1, source_target_pairs={{0,8},{8,0},{16,24},{24,16},{1,9},{9,1},{17,25},{25,17},{2,10},{10... | collective-permute-start | bytes 983048 | tf_op jit(solution)/shard_map/ppermute | solution.py:16
  197.3 2.4 collective-permute-start.47
  201.1 10.1 %collective-permute-done.45 = f32[160,512]{1,0:T(8,128)S(1)} collective-permute-done((f32[160,512]{1,0:T(8,128)S(1)}, f32[160,512]{1,0:T(8,128)S(1)}, u32[]{:S(2)}, u32[]{:S(2)}) %collective-permute-start.45) | collective-permute-done | bytes 327712 | tf_op jit(solution)/shard_map/ppermute | solution.py:16
  211.2 11.7 %collective-permute-done.46 = f32[160,512]{1,0:T(8,128)S(1)} collective-permute-done((f32[160,512]{1,0:T(8,128)S(1)}, f32[160,512]{1,0:T(8,128)S(1)}, u32[]{:S(2)}, u32[]{:S(2)}) %collective-permute-start.46) | collective-permute-done | bytes 327712 | tf_op jit(solution)/shard_map/ppermute | solution.py:16
  224.2 6.5 %collective-permute-start.51 = (bf16[160,512]{1,0:T(8,128)(2,1)S(1)}, bf16[160,512]{1,0:T(8,128)(2,1)S(1)}, u32[]{:S(2)}, u32[]{:S(2)}) collective-permute-start(bf16[160,512]{1,0:T(8,128)(2,1)S(1)} %reduce-precision_convert_fusion.8), channel_id=1, source_target_pairs={{0,16},{8,24},{16,0},{24,8},{1,17},{9,25},{17,1},{25,9},{2,18},{10... | collective-permute-start | bytes 491528 | tf_op jit(solution)/shard_map/ppermute | solution.py:16
  230.7 2.4 collective-permute-start.52
  233.1 9.6 %collective-permute-done.51 = bf16[160,512]{1,0:T(8,128)(2,1)S(1)} collective-permute-done((bf16[160,512]{1,0:T(8,128)(2,1)S(1)}, bf16[160,512]{1,0:T(8,128)(2,1)S(1)}, u32[]{:S(2)}, u32[]{:S(2)}) %collective-permute-start.51) | collective-permute-done | bytes 163872 | tf_op jit(solution)/shard_map/ppermute | solution.py:16
  244.3 1.5 collective-permute-start.49
  247.2 6.3 %collective-permute-done.57.refs_1_ = bf16[320,512]{1,0:T(8,128)(2,1)S(1)} collective-permute-done((bf16[320,512]{1,0:T(8,128)(2,1)S(1)}, bf16[320,512]{1,0:T(8,128)(2,1)S(1)}, u32[]{:S(2)}, u32[]{:S(2)}) %collective-permute-start.57) | collective-permute-done | bytes 327712 | tf_op jit(solution)/shard_map/ppermute | solution.py:16
  255.7 5.0 %collective-permute-done.49.refs_0_ = bf16[320,512]{1,0:T(8,128)(2,1)} collective-permute-done((bf16[320,512]{1,0:T(8,128)(2,1)S(1)}, bf16[320,512]{1,0:T(8,128)(2,1)}, u32[]{:S(2)}, u32[]{:S(2)}) %collective-permute-start.49) | collective-permute-done | bytes 327712 | tf_op jit(solution)/shard_map/ppermute | solution.py:16
  262.0 5.1 %collective-permute-done.54.refs_1_ = bf16[320,512]{1,0:T(8,128)(2,1)S(1)} collective-permute-done((bf16[320,512]{1,0:T(8,128)(2,1)}, bf16[320,512]{1,0:T(8,128)(2,1)S(1)}, u32[]{:S(2)}, u32[]{:S(2)}) %collective-permute-start.54) | collective-permute-done | bytes 327712 | tf_op jit(solution)/shard_map/ppermute | solution.py:16
  267.1 2.6 collective-permute-done.50.refs_0_
  271.3 3.8 %all-to-all-start = ((f32[2,8,20,512]{3,0,2,1:T(2,128)}), f32[2,8,20,512]{3,0,2,1:T(2,128)S(1)}, u32[]{:S(2)}, u32[]{:S(2)}) async-start(f32[2,8,20,512]{3,0,2,1:T(2,128)} %copy.49), calls=%async_computation | async-start | bytes 1310720 | tf_op jit(solution)/shard_map/all_to_all | solution.py:288
  275.1 4.1 %apply.9.refs_12_ = f32[640,512]{1,0:T(8,128)} custom-call(s32[2]{0:T(128)} %iota_xor_fusion.where_ref, bf16[320,512]{1,0:T(8,128)(2,1)} %copy-done.10, bf16[320,512]{1,0:T(8,128)(2,1)} %copy-done.19, bf16[320,512]{1,0:T(8,128)(2,1)} %copy-done.35, bf16[320,512]{1,0:T(8,128)(2,1)} %copy-done.34, ...), custom_call_target="tpu_custom_call" | custom-call | flops 671088640 | bytes 3145728 | tf_op jit(solution)/shard_map/apply/pallas_call | solution.py:160
  279.2 2.4 collective-permute-start.65
  284.2 5.7 %apply.10.refs_6_ = f32[640,512]{1,0:T(8,128)} custom-call(s32[4]{0:T(128)} %broadcast_xor_fusion.where_ref, bf16[320,512]{1,0:T(8,128)(2,1)} %collective-permute-done.49.refs_0_, bf16[320,512]{1,0:T(8,128)(2,1)} %copy-done.36, bf16[320,512]{1,0:T(8,128)(2,1)} %collective-permute-done.58.refs_2_, bf16[320,512]{1,0:T(8,128)(2,1)} %copy-done.37, ...), custom_call_target="tpu_custom_call" | custom-call | flops 1342177280 | bytes 6291456 | tf_op jit(solution)/shard_map/apply/pallas_call | solution.py:160
  289.9 4.4 %apply.11 = f32[640,512]{1,0:T(8,128)} custom-call(s32[2]{0:T(128)} %broadcast_xor_fusion.1.where_ref, bf16[320,512]{1,0:T(8,128)(2,1)} %collective-permute-done.50.refs_0_, bf16[320,512]{1,0:T(8,128)(2,1)} %copy-done.33, bf16[320,512]{1,0:T(8,128)(2,1)} %collective-permute-done.55.refs_2_, bf16[320,512]{1,0:T(8,128)(2,1)} %collective-permute-done.56.refs_3_, ...), custom_call_target="tpu_custom_call" | custom-call | flops 671088640 | bytes 3145728 | tf_op jit(solution)/shard_map/apply/pallas_call | solution.py:160
  294.3 2.4 collective-permute-done.66
  296.7 1.6 multiply_reduce_fusion
  299.9 6.3 %all-to-all-start.1 = ((f32[32,1,20]{2,1,0:T(1,128)}), f32[32,1,20]{2,1,0:T(1,128)S(1)}, u32[]{:S(2)}, u32[]{:S(2)}) async-start(f32[32,1,20]{2,1,0:T(1,128)} %bitcast.15), calls=%async_computation.1 | async-start | bytes 32768 | tf_op jit(solution)/shard_map/all_to_all | solution.py:290
  306.8 6.5 %all-to-all-done.1 = f32[32,1,20]{2,1,0:T(1,128)S(1)} async-done(((f32[32,1,20]{2,1,0:T(1,128)}), f32[32,1,20]{2,1,0:T(1,128)S(1)}, u32[]{:S(2)}, u32[]{:S(2)}) %all-to-all-start.1) | async-done | bytes 2592 | tf_op jit(solution)/shard_map/all_to_all | solution.py:290
  (249 shorter events, 48.9 us)
Async XLA Ops:
  1.4 26.3 %collective-permute-start.12 = (bf16[1,512,640]{2,1,0:T(8,128)(2,1)S(1)}, bf16[1,512,640]{2,1,0:T(8,128)(2,1)}, u32[]{:S(2)}, u32[]{:S(2)}) collective-permute-start(bf16[1,512,640]{2,1,0:T(8,128)(2,1)S(1)} %get-tuple-element.43.refs_2_), channel_id=1, source_target_pairs={{0,1},{1,0},{2,3},{3,2},{4,5},{5,4},{6,7},{7,6},{8,9},{9,8},{10,11... | collective-permute-start | bytes 1966088 | tf_op jit(solution)/shard_map/ppermute | solution.py:16
  2.0 27.2 %collective-permute-start.2 = (bf16[1,512,640]{2,1,0:T(8,128)(2,1)S(1)}, bf16[1,512,640]{2,1,0:T(8,128)(2,1)S(1)}, u32[]{:S(2)}, u32[]{:S(2)}) collective-permute-start(bf16[1,512,640]{2,1,0:T(8,128)(2,1)S(1)} %get-tuple-element.42.refs_3_), channel_id=1, source_target_pairs={{0,4},{1,5},{2,6},{3,7},{4,0},{5,1},{6,2},{7,3},{8,12},{9,13},{10,... | collective-permute-start | bytes 1966088 | tf_op jit(solution)/shard_map/ppermute | solution.py:16
  22.3 19.2 %collective-permute-start.13 = (bf16[1,512,640]{2,1,0:T(8,128)(2,1)S(1)}, bf16[1,512,640]{2,1,0:T(8,128)(2,1)S(1)}, u32[]{:S(2)}, u32[]{:S(2)}) collective-permute-start(bf16[1,512,640]{2,1,0:T(8,128)(2,1)S(1)} %get-tuple-element.42.refs_3_), channel_id=1, source_target_pairs={{0,1},{1,0},{2,3},{3,2},{4,5},{5,4},{6,7},{7,6},{8,9},{9,8},{10,11... | collective-permute-start | bytes 1966088 | tf_op jit(solution)/shard_map/ppermute | solution.py:16
  23.9 17.6 %collective-permute-start = (bf16[1,512,640]{2,1,0:T(8,128)(2,1)S(1)}, bf16[1,512,640]{2,1,0:T(8,128)(2,1)S(1)}, u32[]{:S(2)}, u32[]{:S(2)}) collective-permute-start(bf16[1,512,640]{2,1,0:T(8,128)(2,1)S(1)} %get-tuple-element.43.refs_2_), channel_id=1, source_target_pairs={{0,2},{1,3},{2,0},{3,1},{4,6},{5,7},{6,4},{7,5},{8,10},{9,11},{10,... | collective-permute-start | bytes 1966088 | tf_op jit(solution)/shard_map/ppermute | solution.py:16
  27.2 15.0 %collective-permute-start.9 = (bf16[1,512,640]{2,1,0:T(8,128)(2,1)S(1)}, bf16[1,512,640]{2,1,0:T(8,128)(2,1)S(1)}, u32[]{:S(2)}, u32[]{:S(2)}) collective-permute-start(bf16[1,512,640]{2,1,0:T(8,128)(2,1)S(1)} %get-tuple-element.43.refs_2_), channel_id=1, source_target_pairs={{0,4},{1,5},{2,6},{3,7},{4,0},{5,1},{6,2},{7,3},{8,12},{9,13},{10,... | collective-permute-start | bytes 1966088 | tf_op jit(solution)/shard_map/ppermute | solution.py:16
  27.8 27.9 %collective-permute-start.6 = (bf16[1,512,640]{2,1,0:T(8,128)(2,1)S(1)}, bf16[1,512,640]{2,1,0:T(8,128)(2,1)}, u32[]{:S(2)}, u32[]{:S(2)}) collective-permute-start(bf16[1,512,640]{2,1,0:T(8,128)(2,1)S(1)} %get-tuple-element.42.refs_3_), channel_id=1, source_target_pairs={{0,2},{1,3},{2,0},{3,1},{4,6},{5,7},{6,4},{7,5},{8,10},{9,11},{10,... | collective-permute-start | bytes 1966088 | tf_op jit(solution)/shard_map/ppermute | solution.py:16
  29.2 26.5 %collective-permute-start.11 = (bf16[1,512,640]{2,1,0:T(8,128)(2,1)S(1)}, bf16[1,512,640]{2,1,0:T(8,128)(2,1)S(1)}, u32[]{:S(2)}, u32[]{:S(2)}) collective-permute-start(bf16[1,512,640]{2,1,0:T(8,128)(2,1)S(1)} %collective-permute-done.2.refs_9_), channel_id=1, source_target_pairs={{0,1},{1,0},{2,3},{3,2},{4,5},{5,4},{6,7},{7,6},{8,9},{9,8},{10,11... | collective-permute-start | bytes 1966088 | tf_op jit(solution)/shard_map/ppermute | solution.py:16
  41.5 26.3 %collective-permute-start.7 = (bf16[1,512,640]{2,1,0:T(8,128)(2,1)S(1)}, bf16[1,512,640]{2,1,0:T(8,128)(2,1)}, u32[]{:S(2)}, u32[]{:S(2)}) collective-permute-start(bf16[1,512,640]{2,1,0:T(8,128)(2,1)S(1)} %collective-permute-done.refs_4_), channel_id=1, source_target_pairs={{0,1},{1,0},{2,3},{3,2},{4,5},{5,4},{6,7},{7,6},{8,9},{9,8},{10,11... | collective-permute-start | bytes 1966088 | tf_op jit(solution)/shard_map/ppermute | solution.py:16
  41.5 23.2 %collective-permute-start.1 = (bf16[1,512,640]{2,1,0:T(8,128)(2,1)S(1)}, bf16[1,512,640]{2,1,0:T(8,128)(2,1)}, u32[]{:S(2)}, u32[]{:S(2)}) collective-permute-start(bf16[1,512,640]{2,1,0:T(8,128)(2,1)S(1)} %collective-permute-done.refs_4_), channel_id=1, source_target_pairs={{0,4},{1,5},{2,6},{3,7},{4,0},{5,1},{6,2},{7,3},{8,12},{9,13},{10,... | collective-permute-start | bytes 1966088 | tf_op jit(solution)/shard_map/ppermute | solution.py:16
  42.3 25.5 %collective-permute-start.3 = (bf16[1,512,640]{2,1,0:T(8,128)(2,1)S(1)}, bf16[1,512,640]{2,1,0:T(8,128)(2,1)}, u32[]{:S(2)}, u32[]{:S(2)}) collective-permute-start(bf16[1,512,640]{2,1,0:T(8,128)(2,1)S(1)} %collective-permute-done.2.refs_9_), channel_id=1, source_target_pairs={{0,2},{1,3},{2,0},{3,1},{4,6},{5,7},{6,4},{7,5},{8,10},{9,11},{10,... | collective-permute-start | bytes 1966088 | tf_op jit(solution)/shard_map/ppermute | solution.py:16
  55.7 12.1 %collective-permute-start.10 = (bf16[1,512,640]{2,1,0:T(8,128)(2,1)S(1)}, bf16[1,512,640]{2,1,0:T(8,128)(2,1)S(1)}, u32[]{:S(2)}, u32[]{:S(2)}) collective-permute-start(bf16[1,512,640]{2,1,0:T(8,128)(2,1)S(1)} %collective-permute-done.9.refs_8_), channel_id=1, source_target_pairs={{0,1},{1,0},{2,3},{3,2},{4,5},{5,4},{6,7},{7,6},{8,9},{9,8},{10,11... | collective-permute-start | bytes 1966088 | tf_op jit(solution)/shard_map/ppermute | solution.py:16
  56.5 11.3 %collective-permute-start.8 = (bf16[1,512,640]{2,1,0:T(8,128)(2,1)}, bf16[1,512,640]{2,1,0:T(8,128)(2,1)S(1)}, u32[]{:S(2)}, u32[]{:S(2)}) collective-permute-start(bf16[1,512,640]{2,1,0:T(8,128)(2,1)} %collective-permute-done.6.refs_5_), channel_id=1, source_target_pairs={{0,1},{1,0},{2,3},{3,2},{4,5},{5,4},{6,7},{7,6},{8,9},{9,8},{10,11... | collective-permute-start | bytes 1966088 | tf_op jit(solution)/shard_map/ppermute | solution.py:16
  64.8 17.1 %collective-permute-start.4 = (bf16[1,512,640]{2,1,0:T(8,128)(2,1)}, bf16[1,512,640]{2,1,0:T(8,128)(2,1)}, u32[]{:S(2)}, u32[]{:S(2)}) collective-permute-start(bf16[1,512,640]{2,1,0:T(8,128)(2,1)} %collective-permute-done.1.refs_2_), channel_id=1, source_target_pairs={{0,1},{1,0},{2,3},{3,2},{4,5},{5,4},{6,7},{7,6},{8,9},{9,8},{10,11... | collective-permute-start | bytes 1966088 | tf_op jit(solution)/shard_map/ppermute | solution.py:16
  67.8 14.1 %collective-permute-start.5 = (bf16[1,512,640]{2,1,0:T(8,128)(2,1)}, bf16[1,512,640]{2,1,0:T(8,128)(2,1)S(1)}, u32[]{:S(2)}, u32[]{:S(2)}) collective-permute-start(bf16[1,512,640]{2,1,0:T(8,128)(2,1)} %collective-permute-done.3.refs_3_), channel_id=1, source_target_pairs={{0,1},{1,0},{2,3},{3,2},{4,5},{5,4},{6,7},{7,6},{8,9},{9,8},{10,11... | collective-permute-start | bytes 1966088 | tf_op jit(solution)/shard_map/ppermute | solution.py:16
  91.8 19.7 %collective-permute-start.17 = (f32[160,512]{1,0:T(8,128)S(1)}, f32[160,512]{1,0:T(8,128)S(1)}, u32[]{:S(2)}, u32[]{:S(2)}) collective-permute-start(f32[160,512]{1,0:T(8,128)S(1)} %get-tuple-element.39), channel_id=1, source_target_pairs={{0,8},{8,0},{16,24},{24,16},{1,9},{9,1},{17,25},{25,17},{2,10},{10... | collective-permute-start | bytes 983048 | tf_op jit(solution)/shard_map/ppermute | solution.py:16
  92.6 26.1 %collective-permute-start.18 = (f32[160,512]{1,0:T(8,128)S(1)}, f32[160,512]{1,0:T(8,128)S(1)}, u32[]{:S(2)}, u32[]{:S(2)}) collective-permute-start(f32[160,512]{1,0:T(8,128)S(1)} %get-tuple-element.41), channel_id=1, source_target_pairs={{0,16},{8,24},{16,0},{24,8},{1,17},{9,25},{17,1},{25,9},{2,18},{10... | collective-permute-start | bytes 983048 | tf_op jit(solution)/shard_map/ppermute | solution.py:16
  96.0 22.7 %collective-permute-start.19 = (f32[160,512]{1,0:T(8,128)S(1)}, f32[160,512]{1,0:T(8,128)S(1)}, u32[]{:S(2)}, u32[]{:S(2)}) collective-permute-start(f32[160,512]{1,0:T(8,128)S(1)} %get-tuple-element.40), channel_id=1, source_target_pairs={{0,24},{8,16},{16,8},{24,0},{1,25},{9,17},{17,9},{25,1},{2,26},{10... | collective-permute-start | bytes 983048 | tf_op jit(solution)/shard_map/ppermute | solution.py:16
  119.9 20.3 %collective-permute-start.23 = (f16[160,512]{1,0:T(8,128)(2,1)S(1)}, f16[160,512]{1,0:T(8,128)(2,1)S(1)}, u32[]{:S(2)}, u32[]{:S(2)}) collective-permute-start(f16[160,512]{1,0:T(8,128)(2,1)S(1)} %get-tuple-element.34), channel_id=1, source_target_pairs={{0,16},{8,24},{16,0},{24,8},{1,17},{9,25},{17,1},{25,9},{2,18},{10... | collective-permute-start | bytes 491528 | tf_op jit(solution)/shard_map/ppermute | solution.py:16
  128.0 12.2 %collective-permute-start.24 = (f16[160,512]{1,0:T(8,128)(2,1)S(1)}, f16[160,512]{1,0:T(8,128)(2,1)S(1)}, u32[]{:S(2)}, u32[]{:S(2)}) collective-permute-start(f16[160,512]{1,0:T(8,128)(2,1)S(1)} %get-tuple-element.34), channel_id=1, source_target_pairs={{0,24},{8,16},{16,8},{24,0},{1,25},{9,17},{17,9},{25,1},{2,26},{10... | collective-permute-start | bytes 491528 | tf_op jit(solution)/shard_map/ppermute | solution.py:16
  129.4 12.8 %collective-permute-start.20 = (f16[160,512]{1,0:T(8,128)(2,1)S(1)}, f16[160,512]{1,0:T(8,128)(2,1)S(1)}, u32[]{:S(2)}, u32[]{:S(2)}) collective-permute-start(f16[160,512]{1,0:T(8,128)(2,1)S(1)} %get-tuple-element.34), channel_id=1, source_target_pairs={{0,8},{8,0},{16,24},{24,16},{1,9},{9,1},{17,25},{25,17},{2,10},{10... | collective-permute-start | bytes 491528 | tf_op jit(solution)/shard_map/ppermute | solution.py:16
  141.8 10.7 %collective-permute-start.25 = (f16[320,512]{1,0:T(8,128)(2,1)S(1)}, f16[320,512]{1,0:T(8,128)(2,1)}, u32[]{:S(2)}, u32[]{:S(2)}) collective-permute-start(f16[320,512]{1,0:T(8,128)(2,1)S(1)} %constant_dynamic-update-slice_fusion), channel_id=1, source_target_pairs={{0,4},{1,5},{2,6},{3,7},{4,0},{5,1},{6,2},{7,3},{8,12},{9,13},{10,... | collective-permute-start | bytes 983048 | tf_op jit(solution)/shard_map/ppermute | solution.py:16
  142.3 12.7 %collective-permute-start.21 = (f16[320,512]{1,0:T(8,128)(2,1)S(1)}, f16[320,512]{1,0:T(8,128)(2,1)}, u32[]{:S(2)}, u32[]{:S(2)}) collective-permute-start(f16[320,512]{1,0:T(8,128)(2,1)S(1)} %pad_maximum_fusion.1), channel_id=1, source_target_pairs={{0,2},{1,3},{2,0},{3,1},{4,6},{5,7},{6,4},{7,5},{8,10},{9,11},{10,... | collective-permute-start | bytes 983048 | tf_op jit(solution)/shard_map/ppermute | solution.py:16
  143.0 17.2 %collective-permute-start.34 = (f16[320,512]{1,0:T(8,128)(2,1)S(1)}, f16[320,512]{1,0:T(8,128)(2,1)}, u32[]{:S(2)}, u32[]{:S(2)}) collective-permute-start(f16[320,512]{1,0:T(8,128)(2,1)S(1)} %pad_maximum_fusion.1), channel_id=1, source_target_pairs={{0,4},{1,5},{2,6},{3,7},{4,0},{5,1},{6,2},{7,3},{8,12},{9,13},{10,... | collective-permute-start | bytes 983048 | tf_op jit(solution)/shard_map/ppermute | solution.py:16
  144.8 12.8 %collective-permute-start.41 = (bf16[320,512]{1,0:T(8,128)(2,1)S(1)}, bf16[320,512]{1,0:T(8,128)(2,1)S(1)}, u32[]{:S(2)}, u32[]{:S(2)}) collective-permute-start(bf16[320,512]{1,0:T(8,128)(2,1)S(1)} %get-tuple-element.49.refs_0_), channel_id=1, source_target_pairs={{0,1},{1,0},{2,3},{3,2},{4,5},{5,4},{6,7},{7,6},{8,9},{9,8},{10,11... | collective-permute-start | bytes 983048 | tf_op jit(solution)/shard_map/ppermute | solution.py:16
  172.4 11.6 %collective-permute-start.28 = (bf16[320,512]{1,0:T(8,128)(2,1)S(1)}, bf16[320,512]{1,0:T(8,128)(2,1)S(1)}, u32[]{:S(2)}, u32[]{:S(2)}) collective-permute-start(bf16[320,512]{1,0:T(8,128)(2,1)S(1)} %get-tuple-element.59.refs_1_), channel_id=1, source_target_pairs={{0,1},{1,0},{2,3},{3,2},{4,5},{5,4},{6,7},{7,6},{8,9},{9,8},{10,11... | collective-permute-start | bytes 983048 | tf_op jit(solution)/shard_map/ppermute | solution.py:16
  172.9 11.0 %collective-permute-start.30 = (bf16[320,512]{1,0:T(8,128)(2,1)S(1)}, bf16[320,512]{1,0:T(8,128)(2,1)S(1)}, u32[]{:S(2)}, u32[]{:S(2)}) collective-permute-start(bf16[320,512]{1,0:T(8,128)(2,1)S(1)} %get-tuple-element.58.refs_5_), channel_id=1, source_target_pairs={{0,1},{1,0},{2,3},{3,2},{4,5},{5,4},{6,7},{7,6},{8,9},{9,8},{10,11... | collective-permute-start | bytes 983048 | tf_op jit(solution)/shard_map/ppermute | solution.py:16
  173.0 11.0 %collective-permute-start.27 = (bf16[320,512]{1,0:T(8,128)(2,1)S(1)}, bf16[320,512]{1,0:T(8,128)(2,1)}, u32[]{:S(2)}, u32[]{:S(2)}) collective-permute-start(bf16[320,512]{1,0:T(8,128)(2,1)S(1)} %get-tuple-element.61.refs_0_), channel_id=1, source_target_pairs={{0,1},{1,0},{2,3},{3,2},{4,5},{5,4},{6,7},{7,6},{8,9},{9,8},{10,11... | collective-permute-start | bytes 983048 | tf_op jit(solution)/shard_map/ppermute | solution.py:16
  193.2 17.9 %collective-permute-start.45 = (f32[160,512]{1,0:T(8,128)S(1)}, f32[160,512]{1,0:T(8,128)S(1)}, u32[]{:S(2)}, u32[]{:S(2)}) collective-permute-start(f32[160,512]{1,0:T(8,128)S(1)} %get-tuple-element.36), channel_id=1, source_target_pairs={{0,8},{8,0},{16,24},{24,16},{1,9},{9,1},{17,25},{25,17},{2,10},{10... | collective-permute-start | bytes 983048 | tf_op jit(solution)/shard_map/ppermute | solution.py:16
  197.3 25.5 %collective-permute-start.46 = (f32[160,512]{1,0:T(8,128)S(1)}, f32[160,512]{1,0:T(8,128)S(1)}, u32[]{:S(2)}, u32[]{:S(2)}) collective-permute-start(f32[160,512]{1,0:T(8,128)S(1)} %get-tuple-element.38), channel_id=1, source_target_pairs={{0,16},{8,24},{16,0},{24,8},{1,17},{9,25},{17,1},{25,9},{2,18},{10... | collective-permute-start | bytes 983048 | tf_op jit(solution)/shard_map/ppermute | solution.py:16
  197.3 25.5 %collective-permute-start.47 = (f32[160,512]{1,0:T(8,128)S(1)}, f32[160,512]{1,0:T(8,128)S(1)}, u32[]{:S(2)}, u32[]{:S(2)}) collective-permute-start(f32[160,512]{1,0:T(8,128)S(1)} %get-tuple-element.37), channel_id=1, source_target_pairs={{0,24},{8,16},{16,8},{24,0},{1,25},{9,17},{17,9},{25,1},{2,26},{10... | collective-permute-start | bytes 983048 | tf_op jit(solution)/shard_map/ppermute | solution.py:16
  224.2 18.6 %collective-permute-start.51 = (bf16[160,512]{1,0:T(8,128)(2,1)S(1)}, bf16[160,512]{1,0:T(8,128)(2,1)S(1)}, u32[]{:S(2)}, u32[]{:S(2)}) collective-permute-start(bf16[160,512]{1,0:T(8,128)(2,1)S(1)} %reduce-precision_convert_fusion.8), channel_id=1, source_target_pairs={{0,16},{8,24},{16,0},{24,8},{1,17},{9,25},{17,1},{25,9},{2,18},{10... | collective-permute-start | bytes 491528 | tf_op jit(solution)/shard_map/ppermute | solution.py:16
  230.7 12.1 %collective-permute-start.52 = (bf16[160,512]{1,0:T(8,128)(2,1)S(1)}, bf16[160,512]{1,0:T(8,128)(2,1)S(1)}, u32[]{:S(2)}, u32[]{:S(2)}) collective-permute-start(bf16[160,512]{1,0:T(8,128)(2,1)S(1)} %reduce-precision_convert_fusion.8), channel_id=1, source_target_pairs={{0,24},{8,16},{16,8},{24,0},{1,25},{9,17},{17,9},{25,1},{2,26},{10... | collective-permute-start | bytes 491528 | tf_op jit(solution)/shard_map/ppermute | solution.py:16
  233.1 11.1 %collective-permute-start.48 = (bf16[160,512]{1,0:T(8,128)(2,1)S(1)}, bf16[160,512]{1,0:T(8,128)(2,1)S(1)}, u32[]{:S(2)}, u32[]{:S(2)}) collective-permute-start(bf16[160,512]{1,0:T(8,128)(2,1)S(1)} %reduce-precision_convert_fusion.8), channel_id=1, source_target_pairs={{0,8},{8,0},{16,24},{24,16},{1,9},{9,1},{17,25},{25,17},{2,10},{10... | collective-permute-start | bytes 491528 | tf_op jit(solution)/shard_map/ppermute | solution.py:16
  243.6 10.7 %collective-permute-start.53 = (bf16[320,512]{1,0:T(8,128)(2,1)S(1)}, bf16[320,512]{1,0:T(8,128)(2,1)}, u32[]{:S(2)}, u32[]{:S(2)}) collective-permute-start(bf16[320,512]{1,0:T(8,128)(2,1)S(1)} %constant_dynamic-update-slice_fusion.2.refs_1_), channel_id=1, source_target_pairs={{0,4},{1,5},{2,6},{3,7},{4,0},{5,1},{6,2},{7,3},{8,12},{9,13},{10,... | collective-permute-start | bytes 983048 | tf_op jit(solution)/shard_map/ppermute | solution.py:16
  244.3 16.4 %collective-permute-start.49 = (bf16[320,512]{1,0:T(8,128)(2,1)S(1)}, bf16[320,512]{1,0:T(8,128)(2,1)}, u32[]{:S(2)}, u32[]{:S(2)}) collective-permute-start(bf16[320,512]{1,0:T(8,128)(2,1)S(1)} %pad_maximum_fusion.2.refs_0_), channel_id=1, source_target_pairs={{0,2},{1,3},{2,0},{3,1},{4,6},{5,7},{6,4},{7,5},{8,10},{9,11},{10,... | collective-permute-start | bytes 983048 | tf_op jit(solution)/shard_map/ppermute | solution.py:16
  245.8 15.6 %collective-permute-start.63 = (bf16[320,512]{1,0:T(8,128)(2,1)S(1)}, bf16[320,512]{1,0:T(8,128)(2,1)S(1)}, u32[]{:S(2)}, u32[]{:S(2)}) collective-permute-start(bf16[320,512]{1,0:T(8,128)(2,1)S(1)} %pad_maximum_fusion.2.refs_0_), channel_id=1, source_target_pairs={{0,1},{1,0},{2,3},{3,2},{4,5},{5,4},{6,7},{7,6},{8,9},{9,8},{10,11... | collective-permute-start | bytes 983048 | tf_op jit(solution)/shard_map/ppermute | solution.py:16
  245.8 15.6 %collective-permute-start.60 = (bf16[320,512]{1,0:T(8,128)(2,1)S(1)}, bf16[320,512]{1,0:T(8,128)(2,1)}, u32[]{:S(2)}, u32[]{:S(2)}) collective-permute-start(bf16[320,512]{1,0:T(8,128)(2,1)S(1)} %pad_maximum_fusion.2.refs_0_), channel_id=1, source_target_pairs={{0,4},{1,5},{2,6},{3,7},{4,0},{5,1},{6,2},{7,3},{8,12},{9,13},{10,... | collective-permute-start | bytes 983048 | tf_op jit(solution)/shard_map/ppermute | solution.py:16
  254.3 12.8 %collective-permute-start.54 = (bf16[320,512]{1,0:T(8,128)(2,1)}, bf16[320,512]{1,0:T(8,128)(2,1)S(1)}, u32[]{:S(2)}, u32[]{:S(2)}) collective-permute-start(bf16[320,512]{1,0:T(8,128)(2,1)} %collective-permute-done.53.refs_5_), channel_id=1, source_target_pairs={{0,2},{1,3},{2,0},{3,1},{4,6},{5,7},{6,4},{7,5},{8,10},{9,11},{10,... | collective-permute-start | bytes 983048 | tf_op jit(solution)/shard_map/ppermute | solution.py:16
  261.4 17.8 %collective-permute-start.62 = (bf16[320,512]{1,0:T(8,128)(2,1)}, bf16[320,512]{1,0:T(8,128)(2,1)}, u32[]{:S(2)}, u32[]{:S(2)}) collective-permute-start(bf16[320,512]{1,0:T(8,128)(2,1)} %collective-permute-done.53.refs_5_), channel_id=1, source_target_pairs={{0,1},{1,0},{2,3},{3,2},{4,5},{5,4},{6,7},{7,6},{8,9},{9,8},{10,11... | collective-permute-start | bytes 983048 | tf_op jit(solution)/shard_map/ppermute | solution.py:16
  261.4 20.2 %collective-permute-start.58 = (bf16[320,512]{1,0:T(8,128)(2,1)}, bf16[320,512]{1,0:T(8,128)(2,1)}, u32[]{:S(2)}, u32[]{:S(2)}) collective-permute-start(bf16[320,512]{1,0:T(8,128)(2,1)} %collective-permute-done.49.refs_0_), channel_id=1, source_target_pairs={{0,1},{1,0},{2,3},{3,2},{4,5},{5,4},{6,7},{7,6},{8,9},{9,8},{10,11... | collective-permute-start | bytes 983048 | tf_op jit(solution)/shard_map/ppermute | solution.py:16
  261.9 20.8 %collective-permute-start.61 = (bf16[320,512]{1,0:T(8,128)(2,1)}, bf16[320,512]{1,0:T(8,128)(2,1)}, u32[]{:S(2)}, u32[]{:S(2)}) collective-permute-start(bf16[320,512]{1,0:T(8,128)(2,1)} %collective-permute-done.60.refs_4_), channel_id=1, source_target_pairs={{0,1},{1,0},{2,3},{3,2},{4,5},{5,4},{6,7},{7,6},{8,9},{9,8},{10,11... | collective-permute-start | bytes 983048 | tf_op jit(solution)/shard_map/ppermute | solution.py:16
  267.1 22.8 %collective-permute-start.56 = (bf16[320,512]{1,0:T(8,128)(2,1)S(1)}, bf16[320,512]{1,0:T(8,128)(2,1)}, u32[]{:S(2)}, u32[]{:S(2)}) collective-permute-start(bf16[320,512]{1,0:T(8,128)(2,1)S(1)} %collective-permute-done.54.refs_1_), channel_id=1, source_target_pairs={{0,1},{1,0},{2,3},{3,2},{4,5},{5,4},{6,7},{7,6},{8,9},{9,8},{10,11... | collective-permute-start | bytes 983048 | tf_op jit(solution)/shard_map/ppermute | solution.py:16
  269.7 20.2 %collective-permute-start.55 = (bf16[320,512]{1,0:T(8,128)(2,1)}, bf16[320,512]{1,0:T(8,128)(2,1)}, u32[]{:S(2)}, u32[]{:S(2)}) collective-permute-start(bf16[320,512]{1,0:T(8,128)(2,1)} %collective-permute-done.50.refs_0_), channel_id=1, source_target_pairs={{0,1},{1,0},{2,3},{3,2},{4,5},{5,4},{6,7},{7,6},{8,9},{9,8},{10,11... | collective-permute-start | bytes 983048 | tf_op jit(solution)/shard_map/ppermute | solution.py:16
  271.3 27.1 %all-to-all-start = ((f32[2,8,20,512]{3,0,2,1:T(2,128)}), f32[2,8,20,512]{3,0,2,1:T(2,128)S(1)}, u32[]{:S(2)}, u32[]{:S(2)}) async-start(f32[2,8,20,512]{3,0,2,1:T(2,128)} %copy.49), calls=%async_computation | async-start | bytes 1310720 | tf_op jit(solution)/shard_map/all_to_all | solution.py:288
  279.2 15.1 %collective-permute-start.65 = (bf16[160,512]{1,0:T(8,128)(2,1)S(1)}, bf16[160,512]{1,0:T(8,128)(2,1)S(1)}, u32[]{:S(2)}, u32[]{:S(2)}) collective-permute-start(bf16[160,512]{1,0:T(8,128)(2,1)S(1)} %get-tuple-element.32), channel_id=1, source_target_pairs={{0,8},{8,0},{16,24},{24,16},{1,9},{9,1},{17,25},{25,17},{2,10},{10... | collective-permute-start | bytes 491528 | tf_op jit(solution)/shard_map/ppermute | solution.py:16
  281.7 15.0 %collective-permute-start.66 = (bf16[160,512]{1,0:T(8,128)(2,1)S(1)}, bf16[160,512]{1,0:T(8,128)(2,1)S(1)}, u32[]{:S(2)}, u32[]{:S(2)}) collective-permute-start(bf16[160,512]{1,0:T(8,128)(2,1)S(1)} %get-tuple-element.32), channel_id=1, source_target_pairs={{0,16},{8,24},{16,0},{24,8},{1,17},{9,25},{17,1},{25,9},{2,18},{10... | collective-permute-start | bytes 491528 | tf_op jit(solution)/shard_map/ppermute | solution.py:16
  282.7 14.0 %collective-permute-start.67 = (bf16[160,512]{1,0:T(8,128)(2,1)S(1)}, bf16[160,512]{1,0:T(8,128)(2,1)S(1)}, u32[]{:S(2)}, u32[]{:S(2)}) collective-permute-start(bf16[160,512]{1,0:T(8,128)(2,1)S(1)} %get-tuple-element.32), channel_id=1, source_target_pairs={{0,24},{8,16},{16,8},{24,0},{1,25},{9,17},{17,9},{25,1},{2,26},{10... | collective-permute-start | bytes 491528 | tf_op jit(solution)/shard_map/ppermute | solution.py:16
  299.9 13.4 %all-to-all-start.1 = ((f32[32,1,20]{2,1,0:T(1,128)}), f32[32,1,20]{2,1,0:T(1,128)S(1)}, u32[]{:S(2)}, u32[]{:S(2)}) async-start(f32[32,1,20]{2,1,0:T(1,128)} %bitcast.15), calls=%async_computation.1 | async-start | bytes 32768 | tf_op jit(solution)/shard_map/all_to_all | solution.py:290
  (69 other events, 674.0 us)

commit v3 on v2

--- a/solution.py
+++ b/solution.py
@@ -229,8 +229,10 @@
     facts = sum(others)
     diag = facts[0]
     place = lax.broadcasted_iota(jnp.int32, facts.shape, 0)
+    reach = jnp.max(facts[1])
     facts = jnp.where(place == 0, diag * diag, jnp.where(place == 3, diag * diag * diag, facts))
     facts = jnp.sum(facts, axis=1)
+    facts = jnp.where(lax.iota(jnp.int32, facts.shape[0]) == 1, reach, facts)
     held.update({j ^ 1: piece for j, piece in crossed.items()})
     total = None
     for k, js in enumerate(levels):
@@ -255,9 +257,8 @@
         both = [{**held, **{j ^ 1: piece for j, piece in other.items()}} for held, other in zip(values, crossed)]
         total = None
         for js in levels:
-            before = total
             total = apply([[x[j] for j in js] for x in both], high, low, where(js), total)
-        return before, total
+        return total
 
     def q_of(exact):
         sent = lax.reduce_precision(exact * b_scale, 5, 10)
@@ -265,9 +266,13 @@
         for piece in held.values():
             for p, x in enumerate(piece):
                 piece[p] = split(x.astype(f32))
-        _, total = multiply([{j: [x[i] for x in piece] for j, piece in held.items()} for i in range(2)], low)
+        total = multiply([{j: [x[i] for x in piece] for j, piece in held.items()} for i in range(2)], low)
         lost = exact - sent / b_scale
-        return sum_silos(list(total.reshape(n_silo, small, rows))) / b_scale + diag[None] * lost
+        total = total.reshape(n_silo, small, rows)
+        parts = []
+        for j in range(1, n_silo):
+            parts.append(swap((total[j] / reach).astype(f16), "silo", n_silo, j))
+        return (total[0] + reach * sum(x.astype(f32) for x in parts)) / b_scale + diag[None] * lost
 
     q = [q_of(x) for x in b]
 
@@ -275,17 +280,17 @@
         upper, lower = split(x - shift * y)
         upper, lower = gather_silos(upper), gather_silos(lower)
         held = gather_halves(upper)
-        before = [held[j][0][:8, :128] for j in offsets if bin(j).count("1") == 1]
-        _, total = multiply([held], None)
+        total = multiply([held], None)
         rounded = jnp.concatenate(upper).astype(f32) + 2.0 * jnp.concatenate(lower).astype(f32)
-        return before, jnp.sum(total * rounded, axis=1).reshape(n_silo, small)
+        return jnp.sum(total * rounded, axis=1).reshape(n_silo, small)
 
     curves = [curve_of(x, y) for x, y in zip(b, q)]
-    curved = jnp.concatenate([curve for _, curve in curves], axis=1)
+    curved = jnp.concatenate(curves, axis=1)
     curved = jnp.stack([lax.dynamic_index_in_dim(curved, silo ^ j, axis=0, keepdims=False) for j in range(n_silo)])
-    both = jnp.stack([jnp.concatenate(b), jnp.concatenate(q)]).reshape(2, n_row, served, rows)
-    both, _ = lax.optimization_barrier((both, curves[-1][0]))
-    both = lax.all_to_all(both, "row", split_axis=1, concat_axis=1, tiled=True)
+    both = []
+    for value in (b, q):
+        value = jnp.concatenate(value).reshape(n_row, served, rows)
+        both.append(lax.all_to_all(value, "row", split_axis=0, concat_axis=0, tiled=True))
     both, curved = lax.optimization_barrier((both, curved))
     curved = lax.all_to_all(curved.reshape(n_silo * n_row, served), ("silo", "row"), split_axis=0, concat_axis=0, tiled=True)
     vav = jnp.sum(curved, axis=0)

time: 315 us -> 304 us (0.965)
  waiting for transfers between devices: 118 us -> 110 us
  local copies, waits for them, and re-layouts: 12.8 us -> 9.49 us
    ppermute x68, waiting for transfers between devices: 111 us -> 97.5 us  [swap(): return lax.ppermute(value, axis, [(i, i ^ bit) for i in range(size)])]
    all_to_all x1 -> x2, waiting for transfers between devices: 0.01 us -> 6.52 us  [merge(): lax.all_to_all(value, 'row', split_axis=0, concat_axis=0, tiled=True)]
    all_to_all x1 -> x2, starting transfers between devices: 3.76 us -> 7.58 us  [merge(): lax.all_to_all(value, 'row', split_axis=0, concat_axis=0, tiled=True)]
    all_to_all x1, starting transfers between devices: 6.34 us -> 2.74 us  [merge(): lax.all_to_all(curved.reshape(n_silo * n_row, served), ('silo', 'row'), s...]
  transfers between devices with their start and end apart: 70 -> 71, of which waited for: 23 -> 23; matrix products, arithmetic and copies ran while one was open for 4% -> 5% of each run, Pallas kernels for 20% -> 17%
where the time goes in v3:
time: 304 us; the launch traced here: 303 us
  waiting for transfers between devices  110 us (36%)
  Pallas kernels  77.3 us (25%)
  starting transfers between devices  72.6 us (24%)
  other arithmetic  16.8 us (6%)
  blocking collectives  13.3 us (4%)
  local copies, waits for them, and re-layouts  9.49 us (3%)
  between operations  3.47 us (1%)
    ppermute x68, waiting for transfers between devices, swap(): return lax.ppermute(value, axis, [(i, i ^ bit) for i in range(size)])  97.5 us
    ppermute x68, starting transfers between devices, swap(): return lax.ppermute(value, axis, [(i, i ^ bit) for i in range(size)])  62.3 us
    pallas_call x6, Pallas kernels, apply(): pl.pallas_call(functools.partial(apply_kernel, shape, exact), grid_spec=p...  36.5 us
    pallas_call x3, Pallas kernels, rhs(): pl.pallas_call(functools.partial(rhs_kernel, count, parts, last), grid_sp...  27.8 us
    psum x1, blocking collectives, merge(): table = lax.psum(jnp.where(slot == row, facts[None], 0.0), 'row')  13.3 us
    pallas_call x1, Pallas kernels, prepare(): pl.pallas_call(prepare_kernel, grid_spec=pltpu.PrefetchScalarGridSpec(num...  13 us
    all_to_all x2, starting transfers between devices, merge(): lax.all_to_all(value, 'row', split_axis=0, concat_axis=0, tiled=True)  7.58 us
    convert_element_type x10, other arithmetic, split(): return (high.astype(bf16), (value - high).astype(bf16))  7.49 us
  transfers between devices with their start and end apart: 71, of which 23 were waited for; matrix products, arithmetic and copies ran while one was open for 5% of the time, Pallas kernels for 17%

profile of v3, /device:TPU:0, one launch (start us, length us, event | category | flops | bytes accessed | tf_op | source)
XLA Modules:
  0.0 302.9 jit_solution(8428112062713536365)
XLA Ops:
  0.0 13.0 %prepare.1 = (bf16[4096,512]{1,0:T(8,128)(2,1)}, bf16[4096,512]{1,0:T(8,128)(2,1)}, f32[8,512]{1,0:T(8,128)}) custom-call(s32[1]{0:T(128)} %bitcast.row_ref, f32[2,512,4096]{2,1,0:T(8,128)} %refs_1_.5, bf16[2,512,640]{2,1,0:T(8,128)(2,1)} %weight_ref.1), custom_call_target="tpu_custom_call" | custom-call | flops 1677721600 | bytes 25165824 | tf_op jit(solution)/shard_map/prepare/pallas_call | solution.py:67
  13.0 2.9 collective-permute-start.14
  16.0 2.6 collective-permute-start.15
  18.8 1.8 collective-permute-start.2
  24.3 1.5 collective-permute-start.9
  27.3 9.2 %collective-permute-done.2.refs_9_ = bf16[1,512,640]{2,1,0:T(8,128)(2,1)S(1)} collective-permute-done((bf16[1,512,640]{2,1,0:T(8,128)(2,1)S(1)}, bf16[1,512,640]{2,1,0:T(8,128)(2,1)S(1)}, u32[]{:S(2)}, u32[]{:S(2)}) %collective-permute-start.2) | collective-permute-done | bytes 655392 | tf_op jit(solution)/shard_map/ppermute | solution.py:16
  37.4 2.7 collective-permute-done.refs_4_
  40.4 10.1 %collective-permute-done.9.refs_8_ = bf16[1,512,640]{2,1,0:T(8,128)(2,1)S(1)} collective-permute-done((bf16[1,512,640]{2,1,0:T(8,128)(2,1)S(1)}, bf16[1,512,640]{2,1,0:T(8,128)(2,1)S(1)}, u32[]{:S(2)}, u32[]{:S(2)}) %collective-permute-start.9) | collective-permute-done | bytes 655392 | tf_op jit(solution)/shard_map/ppermute | solution.py:16
  50.5 1.7 collective-permute-start.3
  52.2 2.0 collective-permute-done.6.refs_5_
  56.2 7.5 %rhs.3.refs_12_ = f32[512,640]{1,0:T(8,128)} custom-call(s32[2]{0:T(128)} %iota_xor_fusion.where_ref, f32[2,512,4096]{2,1,0:T(8,128)} %refs_1_.5, f32[2,512,4096]{2,1,0:T(8,128)} %refs_1_.5, bf16[1,512,640]{2,1,0:T(8,128)(2,1)} %copy-done.2, bf16[1,512,640]{2,1,0:T(8,128)(2,1)} %copy-done.1, bf16[1,512,640]{2,1,0:T(8,128)(2,1)} %collective-permute-done.12.refs_4_, ...), custom_call_target="tpu_custom_call" | custom-call | flops 5368709120 | bytes 4194304 | tf_op jit(solution)/shard_map/rhs/pallas_call | solution.py:114
  64.1 3.5 %collective-permute-done.3.refs_3_ = bf16[1,512,640]{2,1,0:T(8,128)(2,1)} collective-permute-done((bf16[1,512,640]{2,1,0:T(8,128)(2,1)S(1)}, bf16[1,512,640]{2,1,0:T(8,128)(2,1)}, u32[]{:S(2)}, u32[]{:S(2)}) %collective-permute-start.3) | collective-permute-done | bytes 655392 | tf_op jit(solution)/shard_map/ppermute | solution.py:16
  67.6 12.4 %rhs.4.refs_6_ = f32[512,640]{1,0:T(8,128)} custom-call(s32[4]{0:T(128)} %broadcast_xor_fusion.where_ref, f32[2,512,4096]{2,1,0:T(8,128)} %refs_1_.5, f32[2,512,4096]{2,1,0:T(8,128)} %refs_1_.5, f32[2,512,4096]{2,1,0:T(8,128)} %refs_1_.5, f32[2,512,4096]{2,1,0:T(8,128)} %refs_1_.5, bf16[1,512,640]{2,1,0:T(8,128)(2,1)} %copy-done.22, ...), custom_call_target="tpu_custom_call" | custom-call | flops 10737418240 | bytes 8388608 | tf_op jit(solution)/shard_map/rhs/pallas_call | solution.py:114
  81.7 7.8 %rhs.5 = f32[640,512]{1,0:T(8,128)} custom-call(s32[2]{0:T(128)} %broadcast_xor_fusion.1.where_ref, f32[2,512,4096]{2,1,0:T(8,128)} %refs_1_.5, f32[2,512,4096]{2,1,0:T(8,128)} %refs_1_.5, bf16[1,512,640]{2,1,0:T(8,128)(2,1)} %collective-permute-done.1.refs_2_, bf16[1,512,640]{2,1,0:T(8,128)(2,1)} %collective-permute-done.3.refs_3_, ...), custom_call_target="tpu_custom_call" | custom-call | flops 5368709120 | bytes 4194304 | tf_op jit(solution)/shard_map/rhs/pallas_call | solution.py:114
  91.5 3.5 %collective-permute-start.18 = (f32[160,512]{1,0:T(8,128)S(1)}, f32[160,512]{1,0:T(8,128)S(1)}, u32[]{:S(2)}, u32[]{:S(2)}) collective-permute-start(f32[160,512]{1,0:T(8,128)S(1)} %get-tuple-element.43), channel_id=1, source_target_pairs={{0,16},{8,24},{16,0},{24,8},{1,17},{9,25},{17,1},{25,9},{2,18},{10... | collective-permute-start | bytes 983048 | tf_op jit(solution)/shard_map/ppermute | solution.py:16
  95.3 13.3 %psum.7 = f32[8,8]{0,1:T(8,128)S(1)} all-reduce(f32[8,8]{0,1:T(8,128)S(1)} %broadcast_select_fusion), channel_id=1, replica_groups=mesh['silo'=4,'row'=8] {'row'}, use_global_device_ids=true, to_apply=%region_2.3 | all-reduce | flops 64 | bytes 512 | tf_op jit(solution)/shard_map/psum | solution.py:243
  110.6 7.1 %collective-permute-done.18 = f32[160,512]{1,0:T(8,128)S(1)} collective-permute-done((f32[160,512]{1,0:T(8,128)S(1)}, f32[160,512]{1,0:T(8,128)S(1)}, u32[]{:S(2)}, u32[]{:S(2)}) %collective-permute-start.18) | collective-permute-done | bytes 327712 | tf_op jit(solution)/shard_map/ppermute | solution.py:16
  118.9 8.2 %collective-permute-start.23 = (f16[160,512]{1,0:T(8,128)(2,1)S(1)}, f16[160,512]{1,0:T(8,128)(2,1)S(1)}, u32[]{:S(2)}, u32[]{:S(2)}) collective-permute-start(f16[160,512]{1,0:T(8,128)(2,1)S(1)} %get-tuple-element.36), channel_id=1, source_target_pairs={{0,16},{8,24},{16,0},{24,8},{1,17},{9,25},{17,1},{25,9},{2,18},{10... | collective-permute-start | bytes 491528 | tf_op jit(solution)/shard_map/ppermute | solution.py:16
  128.4 10.7 %collective-permute-done.23 = f16[160,512]{1,0:T(8,128)(2,1)S(1)} collective-permute-done((f16[160,512]{1,0:T(8,128)(2,1)S(1)}, f16[160,512]{1,0:T(8,128)(2,1)S(1)}, u32[]{:S(2)}, u32[]{:S(2)}) %collective-permute-start.23) | collective-permute-done | bytes 163872 | tf_op jit(solution)/shard_map/ppermute | solution.py:16
  139.2 1.5 collective-permute-start.31
  142.0 1.5 collective-permute-start.34
  143.8 6.0 %collective-permute-done.31 = f16[320,512]{1,0:T(8,128)(2,1)S(1)} collective-permute-done((f16[320,512]{1,0:T(8,128)(2,1)S(1)}, f16[320,512]{1,0:T(8,128)(2,1)S(1)}, u32[]{:S(2)}, u32[]{:S(2)}) %collective-permute-start.31) | collective-permute-done | bytes 327712 | tf_op jit(solution)/shard_map/ppermute | solution.py:16
  151.4 2.6 collective-permute-done.21
  159.6 6.1 %apply.6.refs_24_ = f32[640,512]{1,0:T(8,128)} custom-call(s32[2]{0:T(128)} %iota_xor_fusion.where_ref, bf16[320,512]{1,0:T(8,128)(2,1)} %copy-done.15, bf16[320,512]{1,0:T(8,128)(2,1)} %copy-done.13, bf16[320,512]{1,0:T(8,128)(2,1)} %copy-done.39, bf16[320,512]{1,0:T(8,128)(2,1)} %copy-done.42, bf16[320,512]{1,0:T(8,128)(2,1)} %copy-done.14, ...), custom_call_target="tpu_custom_call" | custom-call | flops 2013265920 | bytes 3145728 | tf_op jit(solution)/shard_map/apply/pallas_call | solution.py:160
  173.1 9.7 %apply.7.refs_12_ = f32[640,512]{1,0:T(8,128)} custom-call(s32[4]{0:T(128)} %broadcast_xor_fusion.where_ref, bf16[320,512]{1,0:T(8,128)(2,1)} %copy-done.8, bf16[320,512]{1,0:T(8,128)(2,1)} %copy-done.4, bf16[320,512]{1,0:T(8,128)(2,1)} %copy-done.30, bf16[320,512]{1,0:T(8,128)(2,1)} %collective-permute-done.33.refs_3_, bf16[320,512]{1,0:T(8,128)(2,1)} %copy-done.10, ...), custom_call_target="tpu_custom_call" | custom-call | flops 4026531840 | bytes 6291456 | tf_op jit(solution)/shard_map/apply/pallas_call | solution.py:160
  184.5 6.4 %apply.8 = f32[640,512]{1,0:T(8,128)} custom-call(s32[2]{0:T(128)} %broadcast_xor_fusion.1.where_ref, bf16[320,512]{1,0:T(8,128)(2,1)} %copy-done.19, bf16[320,512]{1,0:T(8,128)(2,1)} %copy-done.17, bf16[320,512]{1,0:T(8,128)(2,1)} %collective-permute-done.27.refs_2_, bf16[320,512]{1,0:T(8,128)(2,1)} %copy-done.41, bf16[320,512]{1,0:T(8,128)(2,1)} %copy-done.18, ...), custom_call_target="tpu_custom_call" | custom-call | flops 2013265920 | bytes 3145728 | tf_op jit(solution)/shard_map/apply/pallas_call | solution.py:160
  192.2 4.1 %collective-permute-start.45 = (f16[160,512]{1,0:T(8,128)(2,1)S(1)}, f16[160,512]{1,0:T(8,128)(2,1)S(1)}, u32[]{:S(2)}, u32[]{:S(2)}) collective-permute-start(f16[160,512]{1,0:T(8,128)(2,1)S(1)} %get-tuple-element.38), channel_id=1, source_target_pairs={{0,8},{8,0},{16,24},{24,16},{1,9},{9,1},{17,25},{25,17},{2,10},{10... | collective-permute-start | bytes 491528 | tf_op jit(solution)/shard_map/ppermute | solution.py:16
  196.3 2.4 collective-permute-start.47
  200.0 3.1 %collective-permute-done.45 = f16[160,512]{1,0:T(8,128)(2,1)S(1)} collective-permute-done((f16[160,512]{1,0:T(8,128)(2,1)S(1)}, f16[160,512]{1,0:T(8,128)(2,1)S(1)}, u32[]{:S(2)}, u32[]{:S(2)}) %collective-permute-start.45) | collective-permute-done | bytes 163872 | tf_op jit(solution)/shard_map/ppermute | solution.py:16
  203.1 8.2 %collective-permute-done.46 = f16[160,512]{1,0:T(8,128)(2,1)S(1)} collective-permute-done((f16[160,512]{1,0:T(8,128)(2,1)S(1)}, f16[160,512]{1,0:T(8,128)(2,1)S(1)}, u32[]{:S(2)}, u32[]{:S(2)}) %collective-permute-start.46) | collective-permute-done | bytes 163872 | tf_op jit(solution)/shard_map/ppermute | solution.py:16
  212.6 3.0 collective-permute-start.51
  215.7 2.4 collective-permute-start.52
  218.1 9.6 %collective-permute-done.51 = bf16[160,512]{1,0:T(8,128)(2,1)S(1)} collective-permute-done((bf16[160,512]{1,0:T(8,128)(2,1)S(1)}, bf16[160,512]{1,0:T(8,128)(2,1)S(1)}, u32[]{:S(2)}, u32[]{:S(2)}) %collective-permute-start.51) | collective-permute-done | bytes 163872 | tf_op jit(solution)/shard_map/ppermute | solution.py:16
  229.3 1.5 collective-permute-start.49
  232.2 6.3 %collective-permute-done.57.refs_1_ = bf16[320,512]{1,0:T(8,128)(2,1)S(1)} collective-permute-done((bf16[320,512]{1,0:T(8,128)(2,1)S(1)}, bf16[320,512]{1,0:T(8,128)(2,1)S(1)}, u32[]{:S(2)}, u32[]{:S(2)}) %collective-permute-start.57) | collective-permute-done | bytes 327712 | tf_op jit(solution)/shard_map/ppermute | solution.py:16
  240.7 5.0 %collective-permute-done.49.refs_0_ = bf16[320,512]{1,0:T(8,128)(2,1)} collective-permute-done((bf16[320,512]{1,0:T(8,128)(2,1)S(1)}, bf16[320,512]{1,0:T(8,128)(2,1)}, u32[]{:S(2)}, u32[]{:S(2)}) %collective-permute-start.49) | collective-permute-done | bytes 327712 | tf_op jit(solution)/shard_map/ppermute | solution.py:16
  247.0 5.1 %collective-permute-done.54.refs_1_ = bf16[320,512]{1,0:T(8,128)(2,1)S(1)} collective-permute-done((bf16[320,512]{1,0:T(8,128)(2,1)}, bf16[320,512]{1,0:T(8,128)(2,1)S(1)}, u32[]{:S(2)}, u32[]{:S(2)}) %collective-permute-start.54) | collective-permute-done | bytes 327712 | tf_op jit(solution)/shard_map/ppermute | solution.py:16
  252.0 2.5 collective-permute-done.50.refs_0_
  255.4 3.5 %all-to-all-start = ((f32[8,20,512]{2,1,0:T(8,128)}), f32[8,20,512]{2,1,0:T(8,128)S(1)}, u32[]{:S(2)}, u32[]{:S(2)}) async-start(f32[8,20,512]{2,1,0:T(8,128)} %reshape.81), calls=%async_computation | async-start | bytes 786432 | tf_op jit(solution)/shard_map/all_to_all | solution.py:293
  259.7 4.1 %apply.9.refs_12_ = f32[640,512]{1,0:T(8,128)} custom-call(s32[2]{0:T(128)} %iota_xor_fusion.where_ref, bf16[320,512]{1,0:T(8,128)(2,1)} %copy-done.11, bf16[320,512]{1,0:T(8,128)(2,1)} %copy-done.20, bf16[320,512]{1,0:T(8,128)(2,1)} %copy-done.36, bf16[320,512]{1,0:T(8,128)(2,1)} %copy-done.34, ...), custom_call_target="tpu_custom_call" | custom-call | flops 671088640 | bytes 3145728 | tf_op jit(solution)/shard_map/apply/pallas_call | solution.py:160
  263.8 2.5 collective-permute-start.65
  268.8 5.7 %apply.10.refs_6_ = f32[640,512]{1,0:T(8,128)} custom-call(s32[4]{0:T(128)} %broadcast_xor_fusion.where_ref, bf16[320,512]{1,0:T(8,128)(2,1)} %collective-permute-done.49.refs_0_, bf16[320,512]{1,0:T(8,128)(2,1)} %copy-done.37, bf16[320,512]{1,0:T(8,128)(2,1)} %collective-permute-done.58.refs_2_, bf16[320,512]{1,0:T(8,128)(2,1)} %copy-done.38, ...), custom_call_target="tpu_custom_call" | custom-call | flops 1342177280 | bytes 6291456 | tf_op jit(solution)/shard_map/apply/pallas_call | solution.py:160
  274.6 4.4 %apply.11 = f32[640,512]{1,0:T(8,128)} custom-call(s32[2]{0:T(128)} %broadcast_xor_fusion.1.where_ref, bf16[320,512]{1,0:T(8,128)(2,1)} %copy-done.35, bf16[320,512]{1,0:T(8,128)(2,1)} %copy-done.33, bf16[320,512]{1,0:T(8,128)(2,1)} %collective-permute-done.55.refs_2_, bf16[320,512]{1,0:T(8,128)(2,1)} %collective-permute-done.56.refs_3_, ...), custom_call_target="tpu_custom_call" | custom-call | flops 671088640 | bytes 3145728 | tf_op jit(solution)/shard_map/apply/pallas_call | solution.py:160
  279.0 4.1 %all-to-all-start.1 = ((f32[8,20,512]{2,1,0:T(8,128)}), f32[8,20,512]{2,1,0:T(8,128)S(1)}, u32[]{:S(2)}, u32[]{:S(2)}) async-start(f32[8,20,512]{2,1,0:T(8,128)} %reshape.82), calls=%async_computation.1 | async-start | bytes 786432 | tf_op jit(solution)/shard_map/all_to_all | solution.py:293
  283.1 1.6 multiply_reduce_fusion
  284.9 6.5 %all-to-all-done.1 = f32[8,20,512]{2,1,0:T(8,128)S(1)} async-done(((f32[8,20,512]{2,1,0:T(8,128)}), f32[8,20,512]{2,1,0:T(8,128)S(1)}, u32[]{:S(2)}, u32[]{:S(2)}) %all-to-all-start.1) | async-done | bytes 327712 | tf_op jit(solution)/shard_map/all_to_all | solution.py:293
  292.1 2.7 all-to-all-start.2
  296.0 5.9 %all-to-all-done.2 = f32[32,1,20]{2,1,0:T(1,128)S(1)} async-done(((f32[32,1,20]{2,1,0:T(1,128)}), f32[32,1,20]{2,1,0:T(1,128)S(1)}, u32[]{:S(2)}, u32[]{:S(2)}) %all-to-all-start.2) | async-done | bytes 2592 | tf_op jit(solution)/shard_map/all_to_all | solution.py:295
  (254 shorter events, 49.7 us)
Async XLA Ops:
  18.8 17.7 %collective-permute-start.2 = (bf16[1,512,640]{2,1,0:T(8,128)(2,1)S(1)}, bf16[1,512,640]{2,1,0:T(8,128)(2,1)S(1)}, u32[]{:S(2)}, u32[]{:S(2)}) collective-permute-start(bf16[1,512,640]{2,1,0:T(8,128)(2,1)S(1)} %get-tuple-element.44.refs_3_), channel_id=1, source_target_pairs={{0,4},{1,5},{2,6},{3,7},{4,0},{5,1},{6,2},{7,3},{8,12},{9,13},{10,... | collective-permute-start | bytes 1966088 | tf_op jit(solution)/shard_map/ppermute | solution.py:16
  22.2 17.8 %collective-permute-start.13 = (bf16[1,512,640]{2,1,0:T(8,128)(2,1)S(1)}, bf16[1,512,640]{2,1,0:T(8,128)(2,1)S(1)}, u32[]{:S(2)}, u32[]{:S(2)}) collective-permute-start(bf16[1,512,640]{2,1,0:T(8,128)(2,1)S(1)} %get-tuple-element.44.refs_3_), channel_id=1, source_target_pairs={{0,1},{1,0},{2,3},{3,2},{4,5},{5,4},{6,7},{7,6},{8,9},{9,8},{10,11... | collective-permute-start | bytes 1966088 | tf_op jit(solution)/shard_map/ppermute | solution.py:16
  22.4 17.6 %collective-permute-start = (bf16[1,512,640]{2,1,0:T(8,128)(2,1)S(1)}, bf16[1,512,640]{2,1,0:T(8,128)(2,1)S(1)}, u32[]{:S(2)}, u32[]{:S(2)}) collective-permute-start(bf16[1,512,640]{2,1,0:T(8,128)(2,1)S(1)} %get-tuple-element.45.refs_2_), channel_id=1, source_target_pairs={{0,2},{1,3},{2,0},{3,1},{4,6},{5,7},{6,4},{7,5},{8,10},{9,11},{10,... | collective-permute-start | bytes 1966088 | tf_op jit(solution)/shard_map/ppermute | solution.py:16
  24.3 26.2 %collective-permute-start.9 = (bf16[1,512,640]{2,1,0:T(8,128)(2,1)S(1)}, bf16[1,512,640]{2,1,0:T(8,128)(2,1)S(1)}, u32[]{:S(2)}, u32[]{:S(2)}) collective-permute-start(bf16[1,512,640]{2,1,0:T(8,128)(2,1)S(1)} %get-tuple-element.45.refs_2_), channel_id=1, source_target_pairs={{0,4},{1,5},{2,6},{3,7},{4,0},{5,1},{6,2},{7,3},{8,12},{9,13},{10,... | collective-permute-start | bytes 1966088 | tf_op jit(solution)/shard_map/ppermute | solution.py:16
  25.8 28.3 %collective-permute-start.6 = (bf16[1,512,640]{2,1,0:T(8,128)(2,1)S(1)}, bf16[1,512,640]{2,1,0:T(8,128)(2,1)}, u32[]{:S(2)}, u32[]{:S(2)}) collective-permute-start(bf16[1,512,640]{2,1,0:T(8,128)(2,1)S(1)} %get-tuple-element.44.refs_3_), channel_id=1, source_target_pairs={{0,2},{1,3},{2,0},{3,1},{4,6},{5,7},{6,4},{7,5},{8,10},{9,11},{10,... | collective-permute-start | bytes 1966088 | tf_op jit(solution)/shard_map/ppermute | solution.py:16
  36.5 17.7 %collective-permute-start.11 = (bf16[1,512,640]{2,1,0:T(8,128)(2,1)S(1)}, bf16[1,512,640]{2,1,0:T(8,128)(2,1)S(1)}, u32[]{:S(2)}, u32[]{:S(2)}) collective-permute-start(bf16[1,512,640]{2,1,0:T(8,128)(2,1)S(1)} %collective-permute-done.2.refs_9_), channel_id=1, source_target_pairs={{0,1},{1,0},{2,3},{3,2},{4,5},{5,4},{6,7},{7,6},{8,9},{9,8},{10,11... | collective-permute-start | bytes 1966088 | tf_op jit(solution)/shard_map/ppermute | solution.py:16
  40.0 27.6 %collective-permute-start.7 = (bf16[1,512,640]{2,1,0:T(8,128)(2,1)S(1)}, bf16[1,512,640]{2,1,0:T(8,128)(2,1)}, u32[]{:S(2)}, u32[]{:S(2)}) collective-permute-start(bf16[1,512,640]{2,1,0:T(8,128)(2,1)S(1)} %collective-permute-done.refs_4_), channel_id=1, source_target_pairs={{0,1},{1,0},{2,3},{3,2},{4,5},{5,4},{6,7},{7,6},{8,9},{9,8},{10,11... | collective-permute-start | bytes 1966088 | tf_op jit(solution)/shard_map/ppermute | solution.py:16
  40.0 24.1 %collective-permute-start.1 = (bf16[1,512,640]{2,1,0:T(8,128)(2,1)S(1)}, bf16[1,512,640]{2,1,0:T(8,128)(2,1)}, u32[]{:S(2)}, u32[]{:S(2)}) collective-permute-start(bf16[1,512,640]{2,1,0:T(8,128)(2,1)S(1)} %collective-permute-done.refs_4_), channel_id=1, source_target_pairs={{0,4},{1,5},{2,6},{3,7},{4,0},{5,1},{6,2},{7,3},{8,12},{9,13},{10,... | collective-permute-start | bytes 1966088 | tf_op jit(solution)/shard_map/ppermute | solution.py:16
  50.5 17.1 %collective-permute-start.3 = (bf16[1,512,640]{2,1,0:T(8,128)(2,1)S(1)}, bf16[1,512,640]{2,1,0:T(8,128)(2,1)}, u32[]{:S(2)}, u32[]{:S(2)}) collective-permute-start(bf16[1,512,640]{2,1,0:T(8,128)(2,1)S(1)} %collective-permute-done.2.refs_9_), channel_id=1, source_target_pairs={{0,2},{1,3},{2,0},{3,1},{4,6},{5,7},{6,4},{7,5},{8,10},{9,11},{10,... | collective-permute-start | bytes 1966088 | tf_op jit(solution)/shard_map/ppermute | solution.py:16
  54.2 13.4 %collective-permute-start.10 = (bf16[1,512,640]{2,1,0:T(8,128)(2,1)S(1)}, bf16[1,512,640]{2,1,0:T(8,128)(2,1)}, u32[]{:S(2)}, u32[]{:S(2)}) collective-permute-start(bf16[1,512,640]{2,1,0:T(8,128)(2,1)S(1)} %collective-permute-done.9.refs_8_), channel_id=1, source_target_pairs={{0,1},{1,0},{2,3},{3,2},{4,5},{5,4},{6,7},{7,6},{8,9},{9,8},{10,11... | collective-permute-start | bytes 1966088 | tf_op jit(solution)/shard_map/ppermute | solution.py:16
  55.0 12.6 %collective-permute-start.8 = (bf16[1,512,640]{2,1,0:T(8,128)(2,1)}, bf16[1,512,640]{2,1,0:T(8,128)(2,1)}, u32[]{:S(2)}, u32[]{:S(2)}) collective-permute-start(bf16[1,512,640]{2,1,0:T(8,128)(2,1)} %collective-permute-done.6.refs_5_), channel_id=1, source_target_pairs={{0,1},{1,0},{2,3},{3,2},{4,5},{5,4},{6,7},{7,6},{8,9},{9,8},{10,11... | collective-permute-start | bytes 1966088 | tf_op jit(solution)/shard_map/ppermute | solution.py:16
  64.1 15.9 %collective-permute-start.4 = (bf16[1,512,640]{2,1,0:T(8,128)(2,1)}, bf16[1,512,640]{2,1,0:T(8,128)(2,1)S(1)}, u32[]{:S(2)}, u32[]{:S(2)}) collective-permute-start(bf16[1,512,640]{2,1,0:T(8,128)(2,1)} %collective-permute-done.1.refs_2_), channel_id=1, source_target_pairs={{0,1},{1,0},{2,3},{3,2},{4,5},{5,4},{6,7},{7,6},{8,9},{9,8},{10,11... | collective-permute-start | bytes 1966088 | tf_op jit(solution)/shard_map/ppermute | solution.py:16
  67.6 12.4 %collective-permute-start.5 = (bf16[1,512,640]{2,1,0:T(8,128)(2,1)}, bf16[1,512,640]{2,1,0:T(8,128)(2,1)S(1)}, u32[]{:S(2)}, u32[]{:S(2)}) collective-permute-start(bf16[1,512,640]{2,1,0:T(8,128)(2,1)} %collective-permute-done.3.refs_3_), channel_id=1, source_target_pairs={{0,1},{1,0},{2,3},{3,2},{4,5},{5,4},{6,7},{7,6},{8,9},{9,8},{10,11... | collective-permute-start | bytes 1966088 | tf_op jit(solution)/shard_map/ppermute | solution.py:16
  90.8 19.8 %collective-permute-start.17 = (f32[160,512]{1,0:T(8,128)S(1)}, f32[160,512]{1,0:T(8,128)S(1)}, u32[]{:S(2)}, u32[]{:S(2)}) collective-permute-start(f32[160,512]{1,0:T(8,128)S(1)} %get-tuple-element.41), channel_id=1, source_target_pairs={{0,8},{8,0},{16,24},{24,16},{1,9},{9,1},{17,25},{25,17},{2,10},{10... | collective-permute-start | bytes 983048 | tf_op jit(solution)/shard_map/ppermute | solution.py:16
  91.5 26.1 %collective-permute-start.18 = (f32[160,512]{1,0:T(8,128)S(1)}, f32[160,512]{1,0:T(8,128)S(1)}, u32[]{:S(2)}, u32[]{:S(2)}) collective-permute-start(f32[160,512]{1,0:T(8,128)S(1)} %get-tuple-element.43), channel_id=1, source_target_pairs={{0,16},{8,24},{16,0},{24,8},{1,17},{9,25},{17,1},{25,9},{2,18},{10... | collective-permute-start | bytes 983048 | tf_op jit(solution)/shard_map/ppermute | solution.py:16
  95.0 22.6 %collective-permute-start.19 = (f32[160,512]{1,0:T(8,128)S(1)}, f32[160,512]{1,0:T(8,128)S(1)}, u32[]{:S(2)}, u32[]{:S(2)}) collective-permute-start(f32[160,512]{1,0:T(8,128)S(1)} %get-tuple-element.42), channel_id=1, source_target_pairs={{0,24},{8,16},{16,8},{24,0},{1,25},{9,17},{17,9},{25,1},{2,26},{10... | collective-permute-start | bytes 983048 | tf_op jit(solution)/shard_map/ppermute | solution.py:16
  118.9 20.3 %collective-permute-start.23 = (f16[160,512]{1,0:T(8,128)(2,1)S(1)}, f16[160,512]{1,0:T(8,128)(2,1)S(1)}, u32[]{:S(2)}, u32[]{:S(2)}) collective-permute-start(f16[160,512]{1,0:T(8,128)(2,1)S(1)} %get-tuple-element.36), channel_id=1, source_target_pairs={{0,16},{8,24},{16,0},{24,8},{1,17},{9,25},{17,1},{25,9},{2,18},{10... | collective-permute-start | bytes 491528 | tf_op jit(solution)/shard_map/ppermute | solution.py:16
  127.0 12.2 %collective-permute-start.24 = (f16[160,512]{1,0:T(8,128)(2,1)S(1)}, f16[160,512]{1,0:T(8,128)(2,1)S(1)}, u32[]{:S(2)}, u32[]{:S(2)}) collective-permute-start(f16[160,512]{1,0:T(8,128)(2,1)S(1)} %get-tuple-element.36), channel_id=1, source_target_pairs={{0,24},{8,16},{16,8},{24,0},{1,25},{9,17},{17,9},{25,1},{2,26},{10... | collective-permute-start | bytes 491528 | tf_op jit(solution)/shard_map/ppermute | solution.py:16
  128.4 12.9 %collective-permute-start.20 = (f16[160,512]{1,0:T(8,128)(2,1)S(1)}, f16[160,512]{1,0:T(8,128)(2,1)S(1)}, u32[]{:S(2)}, u32[]{:S(2)}) collective-permute-start(f16[160,512]{1,0:T(8,128)(2,1)S(1)} %get-tuple-element.36), channel_id=1, source_target_pairs={{0,8},{8,0},{16,24},{24,16},{1,9},{9,1},{17,25},{25,17},{2,10},{10... | collective-permute-start | bytes 491528 | tf_op jit(solution)/shard_map/ppermute | solution.py:16
  140.7 10.7 %collective-permute-start.25 = (f16[320,512]{1,0:T(8,128)(2,1)S(1)}, f16[320,512]{1,0:T(8,128)(2,1)}, u32[]{:S(2)}, u32[]{:S(2)}) collective-permute-start(f16[320,512]{1,0:T(8,128)(2,1)S(1)} %constant_dynamic-update-slice_fusion), channel_id=1, source_target_pairs={{0,4},{1,5},{2,6},{3,7},{4,0},{5,1},{6,2},{7,3},{8,12},{9,13},{10,... | collective-permute-start | bytes 983048 | tf_op jit(solution)/shard_map/ppermute | solution.py:16
  141.4 12.7 %collective-permute-start.21 = (f16[320,512]{1,0:T(8,128)(2,1)S(1)}, f16[320,512]{1,0:T(8,128)(2,1)}, u32[]{:S(2)}, u32[]{:S(2)}) collective-permute-start(f16[320,512]{1,0:T(8,128)(2,1)S(1)} %pad_maximum_fusion), channel_id=1, source_target_pairs={{0,2},{1,3},{2,0},{3,1},{4,6},{5,7},{6,4},{7,5},{8,10},{9,11},{10,... | collective-permute-start | bytes 983048 | tf_op jit(solution)/shard_map/ppermute | solution.py:16
  142.0 17.1 %collective-permute-start.34 = (f16[320,512]{1,0:T(8,128)(2,1)S(1)}, f16[320,512]{1,0:T(8,128)(2,1)}, u32[]{:S(2)}, u32[]{:S(2)}) collective-permute-start(f16[320,512]{1,0:T(8,128)(2,1)S(1)} %pad_maximum_fusion), channel_id=1, source_target_pairs={{0,4},{1,5},{2,6},{3,7},{4,0},{5,1},{6,2},{7,3},{8,12},{9,13},{10,... | collective-permute-start | bytes 983048 | tf_op jit(solution)/shard_map/ppermute | solution.py:16
  143.8 12.8 %collective-permute-start.41 = (bf16[320,512]{1,0:T(8,128)(2,1)S(1)}, bf16[320,512]{1,0:T(8,128)(2,1)S(1)}, u32[]{:S(2)}, u32[]{:S(2)}) collective-permute-start(bf16[320,512]{1,0:T(8,128)(2,1)S(1)} %get-tuple-element.49.refs_0_), channel_id=1, source_target_pairs={{0,1},{1,0},{2,3},{3,2},{4,5},{5,4},{6,7},{7,6},{8,9},{9,8},{10,11... | collective-permute-start | bytes 983048 | tf_op jit(solution)/shard_map/ppermute | solution.py:16
  171.3 11.6 %collective-permute-start.28 = (bf16[320,512]{1,0:T(8,128)(2,1)S(1)}, bf16[320,512]{1,0:T(8,128)(2,1)S(1)}, u32[]{:S(2)}, u32[]{:S(2)}) collective-permute-start(bf16[320,512]{1,0:T(8,128)(2,1)S(1)} %get-tuple-element.59.refs_1_), channel_id=1, source_target_pairs={{0,1},{1,0},{2,3},{3,2},{4,5},{5,4},{6,7},{7,6},{8,9},{9,8},{10,11... | collective-permute-start | bytes 983048 | tf_op jit(solution)/shard_map/ppermute | solution.py:16
  171.9 11.0 %collective-permute-start.30 = (bf16[320,512]{1,0:T(8,128)(2,1)S(1)}, bf16[320,512]{1,0:T(8,128)(2,1)S(1)}, u32[]{:S(2)}, u32[]{:S(2)}) collective-permute-start(bf16[320,512]{1,0:T(8,128)(2,1)S(1)} %get-tuple-element.58.refs_5_), channel_id=1, source_target_pairs={{0,1},{1,0},{2,3},{3,2},{4,5},{5,4},{6,7},{7,6},{8,9},{9,8},{10,11... | collective-permute-start | bytes 983048 | tf_op jit(solution)/shard_map/ppermute | solution.py:16
  172.0 11.0 %collective-permute-start.27 = (bf16[320,512]{1,0:T(8,128)(2,1)S(1)}, bf16[320,512]{1,0:T(8,128)(2,1)}, u32[]{:S(2)}, u32[]{:S(2)}) collective-permute-start(bf16[320,512]{1,0:T(8,128)(2,1)S(1)} %get-tuple-element.61.refs_0_), channel_id=1, source_target_pairs={{0,1},{1,0},{2,3},{3,2},{4,5},{5,4},{6,7},{7,6},{8,9},{9,8},{10,11... | collective-permute-start | bytes 983048 | tf_op jit(solution)/shard_map/ppermute | solution.py:16
  192.2 10.9 %collective-permute-start.45 = (f16[160,512]{1,0:T(8,128)(2,1)S(1)}, f16[160,512]{1,0:T(8,128)(2,1)S(1)}, u32[]{:S(2)}, u32[]{:S(2)}) collective-permute-start(f16[160,512]{1,0:T(8,128)(2,1)S(1)} %get-tuple-element.38), channel_id=1, source_target_pairs={{0,8},{8,0},{16,24},{24,16},{1,9},{9,1},{17,25},{25,17},{2,10},{10... | collective-permute-start | bytes 491528 | tf_op jit(solution)/shard_map/ppermute | solution.py:16
  196.3 15.0 %collective-permute-start.46 = (f16[160,512]{1,0:T(8,128)(2,1)S(1)}, f16[160,512]{1,0:T(8,128)(2,1)S(1)}, u32[]{:S(2)}, u32[]{:S(2)}) collective-permute-start(f16[160,512]{1,0:T(8,128)(2,1)S(1)} %get-tuple-element.40), channel_id=1, source_target_pairs={{0,16},{8,24},{16,0},{24,8},{1,17},{9,25},{17,1},{25,9},{2,18},{10... | collective-permute-start | bytes 491528 | tf_op jit(solution)/shard_map/ppermute | solution.py:16
  196.3 15.0 %collective-permute-start.47 = (f16[160,512]{1,0:T(8,128)(2,1)S(1)}, f16[160,512]{1,0:T(8,128)(2,1)S(1)}, u32[]{:S(2)}, u32[]{:S(2)}) collective-permute-start(f16[160,512]{1,0:T(8,128)(2,1)S(1)} %get-tuple-element.39), channel_id=1, source_target_pairs={{0,24},{8,16},{16,8},{24,0},{1,25},{9,17},{17,9},{25,1},{2,26},{10... | collective-permute-start | bytes 491528 | tf_op jit(solution)/shard_map/ppermute | solution.py:16
  212.6 15.1 %collective-permute-start.51 = (bf16[160,512]{1,0:T(8,128)(2,1)S(1)}, bf16[160,512]{1,0:T(8,128)(2,1)S(1)}, u32[]{:S(2)}, u32[]{:S(2)}) collective-permute-start(bf16[160,512]{1,0:T(8,128)(2,1)S(1)} %reduce-precision_convert_fusion.8), channel_id=1, source_target_pairs={{0,16},{8,24},{16,0},{24,8},{1,17},{9,25},{17,1},{25,9},{2,18},{10... | collective-permute-start | bytes 491528 | tf_op jit(solution)/shard_map/ppermute | solution.py:16
  215.7 12.1 %collective-permute-start.52 = (bf16[160,512]{1,0:T(8,128)(2,1)S(1)}, bf16[160,512]{1,0:T(8,128)(2,1)S(1)}, u32[]{:S(2)}, u32[]{:S(2)}) collective-permute-start(bf16[160,512]{1,0:T(8,128)(2,1)S(1)} %reduce-precision_convert_fusion.8), channel_id=1, source_target_pairs={{0,24},{8,16},{16,8},{24,0},{1,25},{9,17},{17,9},{25,1},{2,26},{10... | collective-permute-start | bytes 491528 | tf_op jit(solution)/shard_map/ppermute | solution.py:16
  218.1 11.1 %collective-permute-start.48 = (bf16[160,512]{1,0:T(8,128)(2,1)S(1)}, bf16[160,512]{1,0:T(8,128)(2,1)S(1)}, u32[]{:S(2)}, u32[]{:S(2)}) collective-permute-start(bf16[160,512]{1,0:T(8,128)(2,1)S(1)} %reduce-precision_convert_fusion.8), channel_id=1, source_target_pairs={{0,8},{8,0},{16,24},{24,16},{1,9},{9,1},{17,25},{25,17},{2,10},{10... | collective-permute-start | bytes 491528 | tf_op jit(solution)/shard_map/ppermute | solution.py:16
  227.9 10.7 %collective-permute-start.57 = (bf16[320,512]{1,0:T(8,128)(2,1)S(1)}, bf16[320,512]{1,0:T(8,128)(2,1)S(1)}, u32[]{:S(2)}, u32[]{:S(2)}) collective-permute-start(bf16[320,512]{1,0:T(8,128)(2,1)S(1)} %constant_dynamic-update-slice_fusion.2.refs_1_), channel_id=1, source_target_pairs={{0,2},{1,3},{2,0},{3,1},{4,6},{5,7},{6,4},{7,5},{8,10},{9,11},{10,... | collective-permute-start | bytes 983048 | tf_op jit(solution)/shard_map/ppermute | solution.py:16
  228.6 10.7 %collective-permute-start.53 = (bf16[320,512]{1,0:T(8,128)(2,1)S(1)}, bf16[320,512]{1,0:T(8,128)(2,1)}, u32[]{:S(2)}, u32[]{:S(2)}) collective-permute-start(bf16[320,512]{1,0:T(8,128)(2,1)S(1)} %constant_dynamic-update-slice_fusion.2.refs_1_), channel_id=1, source_target_pairs={{0,4},{1,5},{2,6},{3,7},{4,0},{5,1},{6,2},{7,3},{8,12},{9,13},{10,... | collective-permute-start | bytes 983048 | tf_op jit(solution)/shard_map/ppermute | solution.py:16
  229.3 16.4 %collective-permute-start.49 = (bf16[320,512]{1,0:T(8,128)(2,1)S(1)}, bf16[320,512]{1,0:T(8,128)(2,1)}, u32[]{:S(2)}, u32[]{:S(2)}) collective-permute-start(bf16[320,512]{1,0:T(8,128)(2,1)S(1)} %pad_maximum_fusion.1.refs_0_), channel_id=1, source_target_pairs={{0,2},{1,3},{2,0},{3,1},{4,6},{5,7},{6,4},{7,5},{8,10},{9,11},{10,... | collective-permute-start | bytes 983048 | tf_op jit(solution)/shard_map/ppermute | solution.py:16
  230.8 15.6 %collective-permute-start.63 = (bf16[320,512]{1,0:T(8,128)(2,1)S(1)}, bf16[320,512]{1,0:T(8,128)(2,1)S(1)}, u32[]{:S(2)}, u32[]{:S(2)}) collective-permute-start(bf16[320,512]{1,0:T(8,128)(2,1)S(1)} %pad_maximum_fusion.1.refs_0_), channel_id=1, source_target_pairs={{0,1},{1,0},{2,3},{3,2},{4,5},{5,4},{6,7},{7,6},{8,9},{9,8},{10,11... | collective-permute-start | bytes 983048 | tf_op jit(solution)/shard_map/ppermute | solution.py:16
  230.8 15.6 %collective-permute-start.60 = (bf16[320,512]{1,0:T(8,128)(2,1)S(1)}, bf16[320,512]{1,0:T(8,128)(2,1)}, u32[]{:S(2)}, u32[]{:S(2)}) collective-permute-start(bf16[320,512]{1,0:T(8,128)(2,1)S(1)} %pad_maximum_fusion.1.refs_0_), channel_id=1, source_target_pairs={{0,4},{1,5},{2,6},{3,7},{4,0},{5,1},{6,2},{7,3},{8,12},{9,13},{10,... | collective-permute-start | bytes 983048 | tf_op jit(solution)/shard_map/ppermute | solution.py:16
  239.3 12.8 %collective-permute-start.54 = (bf16[320,512]{1,0:T(8,128)(2,1)}, bf16[320,512]{1,0:T(8,128)(2,1)S(1)}, u32[]{:S(2)}, u32[]{:S(2)}) collective-permute-start(bf16[320,512]{1,0:T(8,128)(2,1)} %collective-permute-done.53.refs_5_), channel_id=1, source_target_pairs={{0,2},{1,3},{2,0},{3,1},{4,6},{5,7},{6,4},{7,5},{8,10},{9,11},{10,... | collective-permute-start | bytes 983048 | tf_op jit(solution)/shard_map/ppermute | solution.py:16
  246.4 17.4 %collective-permute-start.62 = (bf16[320,512]{1,0:T(8,128)(2,1)}, bf16[320,512]{1,0:T(8,128)(2,1)}, u32[]{:S(2)}, u32[]{:S(2)}) collective-permute-start(bf16[320,512]{1,0:T(8,128)(2,1)} %collective-permute-done.53.refs_5_), channel_id=1, source_target_pairs={{0,1},{1,0},{2,3},{3,2},{4,5},{5,4},{6,7},{7,6},{8,9},{9,8},{10,11... | collective-permute-start | bytes 983048 | tf_op jit(solution)/shard_map/ppermute | solution.py:16
  246.4 19.9 %collective-permute-start.58 = (bf16[320,512]{1,0:T(8,128)(2,1)}, bf16[320,512]{1,0:T(8,128)(2,1)}, u32[]{:S(2)}, u32[]{:S(2)}) collective-permute-start(bf16[320,512]{1,0:T(8,128)(2,1)} %collective-permute-done.49.refs_0_), channel_id=1, source_target_pairs={{0,1},{1,0},{2,3},{3,2},{4,5},{5,4},{6,7},{7,6},{8,9},{9,8},{10,11... | collective-permute-start | bytes 983048 | tf_op jit(solution)/shard_map/ppermute | solution.py:16
  246.9 20.5 %collective-permute-start.61 = (bf16[320,512]{1,0:T(8,128)(2,1)}, bf16[320,512]{1,0:T(8,128)(2,1)}, u32[]{:S(2)}, u32[]{:S(2)}) collective-permute-start(bf16[320,512]{1,0:T(8,128)(2,1)} %collective-permute-done.60.refs_4_), channel_id=1, source_target_pairs={{0,1},{1,0},{2,3},{3,2},{4,5},{5,4},{6,7},{7,6},{8,9},{9,8},{10,11... | collective-permute-start | bytes 983048 | tf_op jit(solution)/shard_map/ppermute | solution.py:16
  252.0 22.5 %collective-permute-start.56 = (bf16[320,512]{1,0:T(8,128)(2,1)S(1)}, bf16[320,512]{1,0:T(8,128)(2,1)}, u32[]{:S(2)}, u32[]{:S(2)}) collective-permute-start(bf16[320,512]{1,0:T(8,128)(2,1)S(1)} %collective-permute-done.54.refs_1_), channel_id=1, source_target_pairs={{0,1},{1,0},{2,3},{3,2},{4,5},{5,4},{6,7},{7,6},{8,9},{9,8},{10,11... | collective-permute-start | bytes 983048 | tf_op jit(solution)/shard_map/ppermute | solution.py:16
  254.5 20.0 %collective-permute-start.55 = (bf16[320,512]{1,0:T(8,128)(2,1)S(1)}, bf16[320,512]{1,0:T(8,128)(2,1)}, u32[]{:S(2)}, u32[]{:S(2)}) collective-permute-start(bf16[320,512]{1,0:T(8,128)(2,1)S(1)} %collective-permute-done.50.refs_0_), channel_id=1, source_target_pairs={{0,1},{1,0},{2,3},{3,2},{4,5},{5,4},{6,7},{7,6},{8,9},{9,8},{10,11... | collective-permute-start | bytes 983048 | tf_op jit(solution)/shard_map/ppermute | solution.py:16
  255.4 23.5 %all-to-all-start = ((f32[8,20,512]{2,1,0:T(8,128)}), f32[8,20,512]{2,1,0:T(8,128)S(1)}, u32[]{:S(2)}, u32[]{:S(2)}) async-start(f32[8,20,512]{2,1,0:T(8,128)} %reshape.81), calls=%async_computation | async-start | bytes 786432 | tf_op jit(solution)/shard_map/all_to_all | solution.py:293
  263.8 19.3 %collective-permute-start.65 = (bf16[160,512]{1,0:T(8,128)(2,1)S(1)}, bf16[160,512]{1,0:T(8,128)(2,1)S(1)}, u32[]{:S(2)}, u32[]{:S(2)}) collective-permute-start(bf16[160,512]{1,0:T(8,128)(2,1)S(1)} %get-tuple-element.34), channel_id=1, source_target_pairs={{0,8},{8,0},{16,24},{24,16},{1,9},{9,1},{17,25},{25,17},{2,10},{10... | collective-permute-start | bytes 491528 | tf_op jit(solution)/shard_map/ppermute | solution.py:16
  266.3 16.8 %collective-permute-start.66 = (bf16[160,512]{1,0:T(8,128)(2,1)S(1)}, bf16[160,512]{1,0:T(8,128)(2,1)S(1)}, u32[]{:S(2)}, u32[]{:S(2)}) collective-permute-start(bf16[160,512]{1,0:T(8,128)(2,1)S(1)} %get-tuple-element.34), channel_id=1, source_target_pairs={{0,16},{8,24},{16,0},{24,8},{1,17},{9,25},{17,1},{25,9},{2,18},{10... | collective-permute-start | bytes 491528 | tf_op jit(solution)/shard_map/ppermute | solution.py:16
  267.4 15.8 %collective-permute-start.67 = (bf16[160,512]{1,0:T(8,128)(2,1)S(1)}, bf16[160,512]{1,0:T(8,128)(2,1)S(1)}, u32[]{:S(2)}, u32[]{:S(2)}) collective-permute-start(bf16[160,512]{1,0:T(8,128)(2,1)S(1)} %get-tuple-element.34), channel_id=1, source_target_pairs={{0,24},{8,16},{16,8},{24,0},{1,25},{9,17},{17,9},{25,1},{2,26},{10... | collective-permute-start | bytes 491528 | tf_op jit(solution)/shard_map/ppermute | solution.py:16
  279.0 12.4 %all-to-all-start.1 = ((f32[8,20,512]{2,1,0:T(8,128)}), f32[8,20,512]{2,1,0:T(8,128)S(1)}, u32[]{:S(2)}, u32[]{:S(2)}) async-start(f32[8,20,512]{2,1,0:T(8,128)} %reshape.82), calls=%async_computation.1 | async-start | bytes 786432 | tf_op jit(solution)/shard_map/all_to_all | solution.py:293
  (72 other events, 731.8 us)
